TPU v7x, 32 devices: a whole 2x2x4 slice. The times are simulated.
32 devices in a mesh: dp: 8 (over y, x, core), tensor: 4 (over z).
Axes of the slice: x: 2, y: 2, z: 4, core: 2. Of those that a mesh axis runs over, the one named last changes fastest.
Arguments:
- tokens: bfloat16 [8, 1024, 1152], P('dp', 'tensor'), may hold values from -6 to 6
- labels: int32 [8], P('dp'), may hold values from 0 to 1000
- timesteps: int32 [8], P('dp'), may hold values from 0 to 999
- label_table: bfloat16 [1001, 1152], replicated, may hold values from -6 to 6
- ada_weight: bfloat16 [1152, 6912], P(None, 'tensor'), may hold values from -0.1875 to 0.1875
- ada_bias: float32 [6912], P('tensor'), may hold values from 0.5 to 1.5
- qkv_weight: bfloat16 [3, 1152, 1152], P(None, None, 'tensor'), may hold values from -0.09375 to 0.09375
- qv_bias: float32 [2, 1152], P(None, 'tensor'), may hold values from -3 to 3
- proj_weight: bfloat16 [1152, 1152], P('tensor'), may hold values from -2 to 2
- out_bias: float32 [2, 1152], replicated, may hold values from -3 to 3
- fc1_weight: bfloat16 [1152, 4608], P(None, 'tensor'), may hold values from -0.1875 to 0.1875
- fc1_bias: float32 [4608], P('tensor'), may hold values from -3 to 3
- fc2_weight: bfloat16 [4608, 1152], P('tensor'), may hold values from -0.09375 to 0.09375
- cotangent: bfloat16 [8, 1024, 1152], P('dp', 'tensor'), may hold values from -6 to 6
Outputs:
- output: bfloat16 [8, 1024, 1152], P('dp', 'tensor')
- input_grad: float32 [8, 1024, 1152], P('dp', 'tensor')
- table_grad: float32 [1001, 1152], replicated
- ada_weight_grad: float32 [1152, 6912], P('dp', 'tensor')
- ada_bias_grad: float32 [6912], P(('tensor', 'dp'))
- qkv_weight_grad: float32 [3, 1152, 1152], P(None, 'dp', 'tensor')
- qv_bias_grad: float32 [2, 1152], replicated
- proj_weight_grad: float32 [1152, 1152], P('tensor', 'dp')
- out_bias_grad: float32 [2, 1152], replicated
- fc1_weight_grad: float32 [1152, 4608], P('dp', 'tensor')
- fc1_bias_grad: float32 [4608], P(('tensor', 'dp'))
- fc2_weight_grad: float32 [4608, 1152], P('tensor', 'dp')
All inputs are finite; a program needn't handle non-finite values.
Results may differ from a plain program's by a relative error of at most 0.018.
Values may be sent and summed in bfloat16 or wider, within the bound.
A program may use at most 192 MiB of HBM per device.

v0:
```python
import math

import jax
import jax.numpy as jnp
from jax import lax
from jax.sharding import PartitionSpec as P

HEAD_DIM = 72
SEQ = 1024


highest = lax.Precision.HIGHEST


def time_features(timesteps, width):
    half = width // 2
    freqs = jnp.exp(-math.log(10000.0) * jnp.arange(half, dtype=jnp.float32) / half)
    angles = timesteps.astype(jnp.float32)[:, None] * freqs[None, :]
    return jnp.concatenate([jnp.cos(angles), jnp.sin(angles)], axis=1)


def normalize(values):
    center = values - jnp.mean(values, axis=-1, keepdims=True)
    spread = jnp.mean(center * center, axis=-1, keepdims=True)
    inv_std = lax.rsqrt(spread + 1e-06)
    return (center * inv_std, inv_std)


def norm_back(grad, normed, inv_std):
    mean_grad = jnp.mean(grad, axis=-1, keepdims=True)
    mean_proj = jnp.mean(grad * normed, axis=-1, keepdims=True)
    return (grad - mean_grad - normed * mean_proj) * inv_std


def body(
    tokens,
    labels,
    timesteps,
    label_table,
    ada_weight,
    ada_bias,
    qkv_weight,
    qv_bias,
    proj_weight,
    out_bias,
    fc1_weight,
    fc1_bias,
    fc2_weight,
    cotangent,
):
    latent_count = tokens.shape[0]
    width = tokens.shape[2]
    tensor_rank = lax.axis_index("tensor")
    head_cols = qkv_weight.shape[2]
    local_heads = head_cols // HEAD_DIM
    block_rows = min(512, SEQ)
    block_count = SEQ // block_rows
    inv_root = 1.0 / math.sqrt(HEAD_DIM)
    cond = label_table[labels].astype(jnp.float32) + time_features(timesteps, width)
    cond_low = jax.nn.silu(cond).astype(jnp.bfloat16)
    mod_part = jnp.dot(cond_low, ada_weight, preferred_element_type=jnp.float32) + ada_bias
    modulation = lax.all_gather(mod_part, "tensor", axis=1, tiled=True)
    shift_attn, scale_attn, gate_attn, shift_mlp, scale_mlp, gate_mlp = [
        piece[:, None, :] for piece in jnp.split(modulation, 6, axis=1)
    ]
    normed_one, inv_one = normalize(tokens.astype(jnp.float32))
    attn_input = (normed_one * (1.0 + scale_attn) + shift_attn).astype(jnp.bfloat16)
    attn_rows = lax.all_gather(attn_input, "tensor", axis=1, tiled=True)
    query = (
        jnp.einsum("lsd,dc->lsc", attn_rows, qkv_weight[0], preferred_element_type=jnp.float32)
        + qv_bias[0]
    ).astype(jnp.bfloat16)
    keyset = jnp.einsum(
        "lsd,dc->lsc", attn_rows, qkv_weight[1], preferred_element_type=jnp.float32
    ).astype(jnp.bfloat16)
    valset = (
        jnp.einsum("lsd,dc->lsc", attn_rows, qkv_weight[2], preferred_element_type=jnp.float32)
        + qv_bias[1]
    ).astype(jnp.bfloat16)
    head_shape = (latent_count, SEQ, local_heads, HEAD_DIM)
    query_heads = query.reshape(head_shape)
    key_heads = keyset.reshape(head_shape)
    val_heads = valset.reshape(head_shape)

    def attend(index):
        start = index * block_rows
        query_block = lax.dynamic_slice_in_dim(query_heads, start, block_rows, axis=1)
        scores = (
            jnp.einsum(
                "lqhd,lkhd->lhqk", query_block, key_heads, preferred_element_type=jnp.float32
            )
            * inv_root
        )
        peak = jnp.max(scores, axis=-1, keepdims=True)
        expd = jnp.exp(scores - peak)
        total = jnp.sum(expd, axis=-1, keepdims=True)
        probs_low = (expd / total).astype(jnp.bfloat16)
        log_total = peak[..., 0] + jnp.log(total[..., 0])
        mixed_block = jnp.einsum(
            "lhqk,lkhd->lqhd", probs_low, val_heads, preferred_element_type=jnp.float32
        ).astype(jnp.bfloat16)
        return (mixed_block, log_total)

    mixed_blocks, log_totals = lax.map(attend, jnp.arange(block_count, dtype=jnp.int32))
    attn_mix = jnp.moveaxis(mixed_blocks, 0, 1).reshape(latent_count, SEQ, head_cols)
    attn_terms = jnp.einsum(
        "lsc,cd->lsd", attn_mix, proj_weight, preferred_element_type=jnp.float32
    )
    attn_branch = (
        lax.psum_scatter(
            attn_terms.astype(jnp.bfloat16), "tensor", scatter_dimension=1, tiled=True
        ).astype(jnp.float32)
        + out_bias[0]
    )
    middle = tokens.astype(jnp.float32) + gate_attn * attn_branch
    normed_two, inv_two = normalize(middle)
    mlp_input = (normed_two * (1.0 + scale_mlp) + shift_mlp).astype(jnp.bfloat16)
    mlp_rows = lax.all_gather(mlp_input, "tensor", axis=1, tiled=True)
    pre_act = (
        jnp.einsum("lsd,dc->lsc", mlp_rows, fc1_weight, preferred_element_type=jnp.float32)
        + fc1_bias
    )
    hidden = jax.nn.gelu(pre_act, approximate=True).astype(jnp.bfloat16)
    mlp_terms = jnp.einsum("lsc,cd->lsd", hidden, fc2_weight, preferred_element_type=jnp.float32)
    mlp_branch = (
        lax.psum_scatter(
            mlp_terms.astype(jnp.bfloat16), "tensor", scatter_dimension=1, tiled=True
        ).astype(jnp.float32)
        + out_bias[1]
    )
    output = (middle + gate_mlp * mlp_branch).astype(jnp.bfloat16)
    out_grad = cotangent.astype(jnp.float32)
    mlp_grad = gate_mlp * out_grad
    gate_mlp_grad = jnp.sum(out_grad * mlp_branch, axis=1)
    mlp_bias_grad = jnp.sum(mlp_grad, axis=(0, 1))
    mlp_grad_rows = lax.all_gather(mlp_grad.astype(jnp.bfloat16), "tensor", axis=1, tiled=True)
    hidden_grad = jnp.einsum(
        "lsd,cd->lsc", mlp_grad_rows, fc2_weight, preferred_element_type=jnp.float32
    )
    unused_value, gelu_pull = jax.vjp(lambda value: jax.nn.gelu(value, approximate=True), pre_act)
    pre_grad = gelu_pull(hidden_grad)[0].astype(jnp.bfloat16)
    fc2_grad = jnp.einsum("lsc,lsd->cd", hidden, mlp_grad_rows, preferred_element_type=jnp.float32)
    fc1_grad = jnp.einsum("lsd,lsc->dc", mlp_rows, pre_grad, preferred_element_type=jnp.float32)
    fc1_bias_grad = jnp.sum(pre_grad, axis=(0, 1), dtype=jnp.float32)
    mlp_back_terms = jnp.einsum(
        "lsc,dc->lsd", pre_grad, fc1_weight, preferred_element_type=jnp.float32
    )
    mlp_back = lax.psum_scatter(
        mlp_back_terms.astype(jnp.bfloat16), "tensor", scatter_dimension=1, tiled=True
    ).astype(jnp.float32)
    shift_mlp_grad = jnp.sum(mlp_back, axis=1)
    scale_mlp_grad = jnp.sum(mlp_back * normed_two, axis=1)
    middle_grad = out_grad + norm_back(mlp_back * (1.0 + scale_mlp), normed_two, inv_two)
    attn_grad = gate_attn * middle_grad
    gate_attn_grad = jnp.sum(middle_grad * attn_branch, axis=1)
    attn_bias_grad = jnp.sum(attn_grad, axis=(0, 1))
    attn_grad_rows = lax.all_gather(attn_grad.astype(jnp.bfloat16), "tensor", axis=1, tiled=True)
    proj_grad = jnp.einsum(
        "lsc,lsd->cd", attn_mix, attn_grad_rows, preferred_element_type=jnp.float32
    )
    mix_grad = jnp.einsum(
        "lsd,cd->lsc", attn_grad_rows, proj_weight, preferred_element_type=jnp.float32
    ).astype(jnp.bfloat16)
    mix_heads = mix_grad.reshape(head_shape)

    def attend_back(carry, index):
        key_total, val_total = carry
        start = index * block_rows
        query_block = lax.dynamic_slice_in_dim(query_heads, start, block_rows, axis=1)
        mix_block = lax.dynamic_slice_in_dim(mix_heads, start, block_rows, axis=1)
        scores = (
            jnp.einsum(
                "lqhd,lkhd->lhqk", query_block, key_heads, preferred_element_type=jnp.float32
            )
            * inv_root
        )
        probs = jnp.exp(scores - log_totals[index][..., None])
        prob_grad = jnp.einsum(
            "lqhd,lkhd->lhqk", mix_block, val_heads, preferred_element_type=jnp.float32
        )
        row_dot = jnp.sum(probs * prob_grad, axis=-1, keepdims=True)
        score_grad = (probs * (prob_grad - row_dot)).astype(jnp.bfloat16)
        query_block_grad = (
            jnp.einsum("lhqk,lkhd->lqhd", score_grad, key_heads, preferred_element_type=jnp.float32)
            * inv_root
        ).astype(jnp.bfloat16)
        key_total = (
            key_total
            + jnp.einsum(
                "lhqk,lqhd->lkhd", score_grad, query_block, preferred_element_type=jnp.float32
            )
            * inv_root
        )
        val_total = val_total + jnp.einsum(
            "lhqk,lqhd->lkhd",
            probs.astype(jnp.bfloat16),
            mix_block,
            preferred_element_type=jnp.float32,
        )
        return ((key_total, val_total), query_block_grad)

    empty = jnp.zeros(head_shape, jnp.float32)
    (key_total, val_total), query_blocks = lax.scan(
        attend_back, (empty, empty), jnp.arange(block_count, dtype=jnp.int32)
    )
    query_grad = jnp.moveaxis(query_blocks, 0, 1).reshape(latent_count, SEQ, head_cols)
    key_grad = key_total.reshape(latent_count, SEQ, head_cols).astype(jnp.bfloat16)
    val_grad = val_total.reshape(latent_count, SEQ, head_cols).astype(jnp.bfloat16)
    qkv_grad = jnp.stack(
        [
            jnp.einsum("lsd,lsc->dc", attn_rows, grad_item, preferred_element_type=jnp.float32)
            for grad_item in (query_grad, key_grad, val_grad)
        ]
    )
    qv_local = jnp.stack(
        [
            jnp.sum(query_grad, axis=(0, 1), dtype=jnp.float32),
            jnp.sum(val_grad, axis=(0, 1), dtype=jnp.float32),
        ]
    )
    attn_back_terms = (
        jnp.einsum("lsc,dc->lsd", query_grad, qkv_weight[0], preferred_element_type=jnp.float32)
        + jnp.einsum("lsc,dc->lsd", key_grad, qkv_weight[1], preferred_element_type=jnp.float32)
        + jnp.einsum("lsc,dc->lsd", val_grad, qkv_weight[2], preferred_element_type=jnp.float32)
    )
    attn_back = lax.psum_scatter(
        attn_back_terms.astype(jnp.bfloat16), "tensor", scatter_dimension=1, tiled=True
    ).astype(jnp.float32)
    shift_attn_grad = jnp.sum(attn_back, axis=1)
    scale_attn_grad = jnp.sum(attn_back * normed_one, axis=1)
    input_grad = middle_grad + norm_back(attn_back * (1.0 + scale_attn), normed_one, inv_one)
    mod_part_grad = jnp.concatenate(
        [
            shift_attn_grad,
            scale_attn_grad,
            gate_attn_grad,
            shift_mlp_grad,
            scale_mlp_grad,
            gate_mlp_grad,
        ],
        axis=1,
    )
    mod_grad = lax.psum(mod_part_grad, "tensor")
    col_count = ada_weight.shape[1]
    mod_cols = lax.dynamic_slice_in_dim(mod_grad, tensor_rank * col_count, col_count, 1)
    ada_grad = jnp.dot(cond_low.astype(jnp.float32).T, mod_cols, precision=highest)
    ada_bias_grad = jnp.sum(mod_cols, axis=0)
    silu_grad = jnp.dot(mod_cols, ada_weight.astype(jnp.float32).T, precision=highest)
    unused_cond, silu_pull = jax.vjp(jax.nn.silu, cond)
    cond_part = silu_pull(silu_grad)[0]
    qv_full = lax.dynamic_update_slice_in_dim(
        jnp.zeros((2, width), jnp.float32), qv_local, tensor_rank * head_cols, 1
    )
    out_bias_part = jnp.stack([attn_bias_grad, mlp_bias_grad])
    class_ids = jnp.arange(label_table.shape[0], dtype=jnp.int32)
    one_hot = (labels[:, None] == class_ids[None, :]).astype(jnp.float32)
    table_part = jnp.dot(one_hot.T, cond_part, precision=highest)
    table_grad, out_bias_grad, qv_bias_grad = lax.psum(
        (table_part, out_bias_part, qv_full), ("dp", "tensor")
    )
    qkv_part, proj_part, fc1_part, fc2_part, ada_part, fc1_bias_part, ada_bias_part = (
        lax.psum_scatter(qkv_grad, "dp", scatter_dimension=1, tiled=True),
        lax.psum_scatter(proj_grad, "dp", scatter_dimension=1, tiled=True),
        lax.psum_scatter(fc1_grad, "dp", scatter_dimension=0, tiled=True),
        lax.psum_scatter(fc2_grad, "dp", scatter_dimension=1, tiled=True),
        lax.psum_scatter(ada_grad, "dp", scatter_dimension=0, tiled=True),
        lax.psum_scatter(fc1_bias_grad, "dp", scatter_dimension=0, tiled=True),
        lax.psum_scatter(ada_bias_grad, "dp", scatter_dimension=0, tiled=True),
    )
    return (
        output,
        input_grad,
        table_grad,
        ada_part,
        ada_bias_part,
        qkv_part,
        qv_bias_grad,
        proj_part,
        out_bias_grad,
        fc1_part,
        fc1_bias_part,
        fc2_part,
    )


def solution(mesh):
    placed = (
        P("dp", "tensor", None),
        P("dp"),
        P("dp"),
        P(),
        P(None, "tensor"),
        P("tensor"),
        P(None, None, "tensor"),
        P(None, "tensor"),
        P("tensor", None),
        P(),
        P(None, "tensor"),
        P("tensor"),
        P("tensor", None),
        P("dp", "tensor", None),
    )
    return jax.shard_map(
        body,
        mesh=mesh,
        in_specs=placed,
        out_specs=(
            P("dp", "tensor", None),
            P("dp", "tensor", None),
            P(),
            P("dp", "tensor"),
            P(("tensor", "dp")),
            P(None, "dp", "tensor"),
            P(),
            P("tensor", "dp"),
            P(),
            P("dp", "tensor"),
            P(("tensor", "dp")),
            P("tensor", "dp"),
        ),
        check_vma=False,
    )
```

profile of v0, /device:TPU:1, one launch (start us, length us, event | category | flops | bytes accessed | tf_op | source)
XLA Modules:
  0.0 982.9 jit_solution(6125443190951422711)
XLA Ops:
  15.6 3.3 convolution_reduce_fusion
  19.0 16.4 %all-reduce = f32[6912]{0:T(1024)S(1)} all-reduce(f32[6912]{0:T(1024)S(1)} %add_dynamic-update-slice_fusion), channel_id=2, replica_groups=mesh['dp'=8,'tensor'=4] {'tensor'}, use_global_device_ids=true, to_apply=%add | all-reduce | flops 6912 | bytes 55296
  37.3 51.9 %all-gather.6.cloned.1.call-done = bf16[1,1024,1152]{2,1,0:T(8,128)(2,1)} async-done(((bf16[1,256,1152]{2,1,0:T(8,128)(2,1)}), bf16[1,1024,1152]{2,1,0:T(8,128)(2,1)}) %all-gather.6.cloned.1.call-update) | async-done | bytes 2359312 | tf_op jit(solution)/shard_map/all_gather | solution.py:68
  89.2 3.7 fusion.104
  92.9 1.8 fusion.98
  94.7 1.8 fusion.101
  97.3 17.3 %while.28 = (s32[]{:T(128)}, bf16[2,1,512,4,72]{2,4,3,1,0:T(8,128)(2,1)}, f32[2,1,4,512]{3,2,1,0:T(4,128)S(1)}, s32[2]{0:T(128)S(1)}, bf16[1,1024,4,72]{1,3,2,0:...) while((s32[]{:T(128)}, ...), condition=%wide.region_5.6_spmd, body=%wide.region_2.5_spmd.sunk | while | flops 622999552 | bytes 34078988 | solution.py:104
  98.6 2.6 multiply_reduce_fusion.7
  101.2 1.8 fusion.184
  103.0 2.2 fusion.185
  107.2 2.6 multiply_reduce_fusion.7
  109.8 1.8 fusion.184
  111.6 2.2 fusion.185
  114.6 1.7 copy.30
  117.3 2.9 fusion.54
  120.4 46.3 %reduce-scatter.12.cloned.1.call-done = bf16[1,256,1152]{2,1,0:T(8,128)(2,1)} async-done(((bf16[1,1024,1152]{2,1,0:T(8,128)(2,1)}), bf16[1,256,1152]{2,1,0:T(8,128)(2,1)}) %reduce-scatter.12.cloned.1.call-update) | async-done | bytes 589840 | tf_op jit(solution)/shard_map/reduce_scatter | solution.py:110
  170.9 2.0 fusion.91
  173.4 47.2 %all-gather.8.cloned.1.call-done = bf16[1,1024,1152]{2,1,0:T(8,128)(2,1)} async-done(((bf16[1,256,1152]{2,1,0:T(8,128)(2,1)}), bf16[1,1024,1152]{2,1,0:T(8,128)(2,1)}) %all-gather.8.cloned.1.call-update) | async-done | bytes 2359312 | tf_op jit(solution)/shard_map/all_gather | solution.py:118
  220.6 8.1 convolution_add_fusion.2
  228.7 42.7 %all-gather.10.cloned.1.call-done = bf16[1,1024,1152]{2,1,0:T(8,128)(2,1)} async-done(((bf16[1,256,1152]{2,1,0:T(8,128)(2,1)}), bf16[1,1024,1152]{2,1,0:T(8,128)(2,1)}) %all-gather.10.cloned.1.call-update) | async-done | bytes 2359312 | tf_op jit(solution)/shard_map/all_gather | solution.py:136
  271.4 9.9 %convert_reduce_fusion = (f32[1152]{0:T(1024)}, bf16[1024,1152]{1,0:T(8,128)(2,1)S(1)}) fusion(f32[1024,1152]{1,0:T(8,128)} %convolution_add_fusion.2, bf16[1152,1152]{1,0:T(8,128)(2,1)S(1)} %copy-done, bf16[1,1024,1152]{2,1,0:T(8,128)(2,1)} %all-gather.10.cloned.1.call-done), kind=kOutput, calls=%fused_computation.62 | convolution fusion | flops 2743860224 | bytes 12096000 | tf_op jit(solution)/shard_map/lsd,cd->lsc/dot_general | solution.py:137
  282.7 4.8 fusion.57
  287.6 7.9 fusion.56
  295.6 38.3 %reduce-scatter.16.cloned.1.call-done = bf16[1,256,1152]{2,1,0:T(8,128)(2,1)} async-done(((bf16[1,1024,1152]{2,1,0:T(8,128)(2,1)}), bf16[1,256,1152]{2,1,0:T(8,128)(2,1)}) %reduce-scatter.16.cloned.1.call-update) | async-done | bytes 589840 | tf_op jit(solution)/shard_map/reduce_scatter | solution.py:148
  333.9 2.4 fusion.121
  336.3 46.9 %reduce-scatter.14.cloned.1.call-done = bf16[1,256,1152]{2,1,0:T(8,128)(2,1)} async-done(((bf16[1,1024,1152]{2,1,0:T(8,128)(2,1)}), bf16[1,256,1152]{2,1,0:T(8,128)(2,1)}) %reduce-scatter.14.cloned.1.call-update) | async-done | bytes 589840 | tf_op jit(solution)/shard_map/reduce_scatter | solution.py:126
  383.2 4.1 multiply_reduce_fusion.4
  388.6 49.5 %all-gather.12.cloned.1.call-done = bf16[1,1024,1152]{2,1,0:T(8,128)(2,1)} async-done(((bf16[1,256,1152]{2,1,0:T(8,128)(2,1)}), bf16[1,1024,1152]{2,1,0:T(8,128)(2,1)}) %all-gather.12.cloned.1.call-update) | async-done | bytes 2359312 | tf_op jit(solution)/shard_map/all_gather | solution.py:157
  438.1 3.6 fusion.107
  442.5 28.8 %while.29 = (s32[]{:T(128)}, f32[1,1024,4,72]{1,3,2,0:T(8,128)S(1)}, f32[1,1024,4,72]{1,3,2,0:T(8,128)}, bf16[2,1,512,4,72]{2,4,3,1,0:T(8,128)(2,1)}, s32[2]{0:T...) while((s32[]{:T(128)}, ...), condition=%wide.region_15.16_spmd.clone, body=%wide.region_13.15_spmd.clone.sunk | while | flops 1536882688 | bytes 89809336 | solution.py:203
  447.2 2.3 fusion.196
  449.4 2.9 multiply_reduce_fusion.8
  452.4 2.1 multiply_convert_fusion.7
  461.6 2.3 fusion.196
  463.8 2.9 multiply_reduce_fusion.8
  466.8 2.1 multiply_convert_fusion.7
  471.5 1.9 copy.31
  473.7 1.5 fusion.127
  475.2 1.5 convolution_add_fusion.1
  476.7 3.0 fusion.55
  480.0 2.7 convolution_bitcast_fusion
  484.8 2.2 pad_maximum_fusion
  487.0 8.6 copy.33
  495.5 9.0 reshape.595
  504.6 1.6 copy-done.53
  506.2 8.1 fusion.62
  514.4 1.6 copy-done.52
  516.0 7.3 fusion.68
  524.3 4.4 fusion.58
  529.1 1.7 fusion.122
  530.9 13.6 %psum.28 = f32[1,6912]{1,0:T(1,128)S(1)} all-reduce(f32[1,6912]{1,0:T(1,128)S(1)} %constant_dynamic-update-slice_fusion), channel_id=1, replica_groups=mesh['dp'=8,'tensor'=4] {'tensor'}, use_global_device_ids=true, to_apply=%region_25.26 | all-reduce | flops 6912 | bytes 55296 | tf_op jit(solution)/shard_map/psum | solution.py:243
  544.5 3.9 convolution_reduce_fusion.1
  548.4 2.5 broadcast_multiply_fusion.1
  551.7 3.8 broadcast_multiply_fusion
  558.6 42.4 %all-reduce.3 = (f32[2,1152]{1,0:T(2,128)}, f32[2,1152]{1,0:T(2,128)}) all-reduce(f32[2,1152]{1,0:T(2,128)S(1)} %dynamic_update_slice.14, f32[2,1152]{1,0:T(2,128)S(1)} %pad_maximum_fusion.1), channel_id=1, replica_groups=mesh['dp'=8,'tensor'=4] {'dp','tensor'}, use_global_device_ids=true, to_apply=%region_32.33 | all-reduce | flops 4608 | bytes 36864 | tf_op jit(solution)/shard_map/psum | solution.py:258
  601.0 22.3 %all-reduce.4 = (f32[1728]{0:T(1024)S(1)}, f32[1152]{0:T(1024)S(1)}) all-reduce(f32[1728]{0:T(1024)S(1)} %dynamic-slice_reduce_fusion, f32[1152]{0:T(1024)S(1)} %copy-done.47), channel_id=8, replica_groups=mesh['dp'=8,'tensor'=4] {'dp'}, use_global_device_ids=true, to_apply=%region_28.29.clone | all-reduce | flops 2880 | bytes 23040
  624.6 1.5 fusion.114
  626.1 1.6 reshape.596
  628.6 13.4 %reduce-scatter.26.cloned.1.call-done = f32[1152,144]{0,1:T(8,128)} async-done(((f32[1152,1152]{0,1:T(8,128)}), f32[1152,144]{0,1:T(8,128)}) %reduce-scatter.26.cloned.1.call-update) | async-done | bytes 663568 | tf_op jit(solution)/shard_map/reduce_scatter | solution.py:265
  642.0 60.9 %reduce-scatter.24.cloned.1.call-done = f32[144,1152]{1,0:T(8,128)} async-done(((f32[1152,1152]{1,0:T(8,128)}), f32[144,1152]{1,0:T(8,128)}) %reduce-scatter.24.cloned.1.call-update) | async-done | bytes 663568 | tf_op jit(solution)/shard_map/reduce_scatter | solution.py:264
  702.9 43.1 %reduce-scatter.22.cloned.1.call-done = f32[288,144]{0,1:T(8,128)} async-done(((f32[288,1152]{0,1:T(8,128)}), f32[288,144]{0,1:T(8,128)}) %reduce-scatter.22.cloned.1.call-update) | async-done | bytes 165904 | tf_op jit(solution)/shard_map/reduce_scatter | solution.py:263
  746.0 150.0 %all-reduce.7.cloned.1.call-done = f32[1001,1152]{1,0:T(8,128)} async-done(((f32[1001,1152]{1,0:T(8,128)}), f32[1001,1152]{1,0:T(8,128)}) %all-reduce.7.cloned.1.call-update) | async-done | bytes 4612624 | tf_op jit(solution)/shard_map/psum | solution.py:258
  896.0 75.0 %reduce-scatter.20.cloned.1.call-done = f32[144,1728]{1,0:T(8,128)} async-done(((f32[1152,1728]{1,0:T(8,128)}), f32[144,1728]{1,0:T(8,128)}) %reduce-scatter.20.cloned.1.call-update) | async-done | bytes 995344 | tf_op jit(solution)/shard_map/reduce_scatter | solution.py:266
  971.0 4.9 copy.72
  (239 shorter events, 39.0 us)
Async XLA Ops:
  7.2 264.2 %copy-start = (bf16[1152,1152]{1,0:T(8,128)(2,1)S(1)}, bf16[1152,1152]{1,0:T(8,128)(2,1)}, u32[]{:S(2)}) copy-start(bf16[1152,1152]{1,0:T(8,128)(2,1)} %param.30) | copy-start | bytes 7962628
  7.2 82.0 %all-gather.6.cloned.1.call-start = ((), (), s32[]{:S(2)}) async-start(), calls=%async_computation.9 | async-start | bytes 2949120 | tf_op jit(solution)/shard_map/all_gather | solution.py:68
  9.9 9.0 copy-start.46
  9.9 25.6 %copy-start.41 = (f32[256]{0:T(256)}, f32[256]{0:T(256)S(1)}, u32[]{:S(2)}) copy-start(f32[256]{0:T(256)S(1)} %broadcast_multiply_fusion.7) | copy-start | bytes 3076
  9.9 26.1 %copy-start.2 = (bf16[1,256,1152]{2,1,0:T(8,128)(2,1)S(1)}, bf16[1,256,1152]{2,1,0:T(8,128)(2,1)}, u32[]{:S(2)}) copy-start(bf16[1,256,1152]{2,1,0:T(8,128)(2,1)} %param.18) | copy-start | bytes 1769476
  11.4 25.8 %copy-start.43 = (f32[256]{0:T(256)}, f32[256]{0:T(256)S(1)}, u32[]{:S(2)}) copy-start(f32[256]{0:T(256)S(1)} %add_rsqrt_fusion.1) | copy-start | bytes 3076
  11.5 2.2 copy-start.32
  11.5 2.1 copy-start.34
  15.5 21.7 %copy-start.48 = (f32[2,288]{1,0:T(2,128)S(1)}, f32[2,288]{1,0:T(2,128)}, u32[]{:S(2)}) copy-start(f32[2,288]{1,0:T(2,128)} %param.25) | copy-start | bytes 6916
  37.2 129.4 %reduce-scatter.12.cloned.1.call-start = ((), (), s32[]{:S(2)}) async-start(), calls=%async_computation.10 | async-start | bytes 2949120 | tf_op jit(solution)/shard_map/reduce_scatter | solution.py:110
  89.2 3.7 copy-start.24
  89.2 3.7 copy-start.50
  101.1 1.8 copy-start.8
  101.1 1.8 copy-start.20
  109.8 1.8 copy-start.8
  109.8 1.8 copy-start.20
  114.6 2.7 copy-start.54
  117.3 3.0 copy-start.45
  120.3 100.4 %all-gather.8.cloned.1.call-start = ((), (), s32[]{:S(2)}) async-start(), calls=%async_computation.11 | async-start | bytes 2949120 | tf_op jit(solution)/shard_map/all_gather | solution.py:118
  166.7 2.9 copy-start.10
  169.6 51.0 %copy-start.55 = (f32[1152]{0:T(1024)S(1)}, f32[1152]{0:T(1024)}, u32[]{:S(2)}) copy-start(f32[1152]{0:T(1024)} %param.29) | copy-start | bytes 13828
  170.9 100.5 %all-gather.10.cloned.1.call-start = ((), (), s32[]{:S(2)}) async-start(), calls=%async_computation.13 | async-start | bytes 2949120 | tf_op jit(solution)/shard_map/all_gather | solution.py:136
  172.9 161.0 %reduce-scatter.16.cloned.1.call-start = ((), (), s32[]{:S(2)}) async-start(), calls=%async_computation.14 | async-start | bytes 2949120 | tf_op jit(solution)/shard_map/reduce_scatter | solution.py:148
  271.4 11.4 %copy-start.49 = (bf16[1152,1152]{1,0:T(8,128)(2,1)S(1)}, bf16[1152,1152]{1,0:T(8,128)(2,1)}, u32[]{:S(2)}) copy-start(bf16[1152,1152]{1,0:T(8,128)(2,1)} %param.28) | copy-start | bytes 7962628
  287.5 95.7 %reduce-scatter.14.cloned.1.call-start = ((), (), s32[]{:S(2)}) async-start(), calls=%async_computation.12 | async-start | bytes 2949120 | tf_op jit(solution)/shard_map/reduce_scatter | solution.py:126
  295.5 38.4 %copy-start.11 = (bf16[1,256,1152]{2,1,0:T(8,128)(2,1)S(1)}, bf16[1,256,1152]{2,1,0:T(8,128)(2,1)}, u32[]{:S(2)}) copy-start(bf16[1,256,1152]{2,1,0:T(8,128)(2,1)} %reduce-scatter.12.cloned.1.call-done) | copy-start | bytes 1769476
  295.5 87.7 %copy-start.22 = (bf16[1,256,1152]{2,1,0:T(8,128)(2,1)S(1)}, bf16[1,256,1152]{2,1,0:T(8,128)(2,1)}, u32[]{:S(2)}) copy-start(bf16[1,256,1152]{2,1,0:T(8,128)(2,1)} %param.31) | copy-start | bytes 1769476
  295.5 142.5 %all-gather.12.cloned.1.call-start = ((), (), s32[]{:S(2)}) async-start(), calls=%async_computation.15 | async-start | bytes 2949120 | tf_op jit(solution)/shard_map/all_gather | solution.py:157
  388.3 140.7 %reduce-scatter.18.cloned.1.call-start = ((), (), s32[]{:S(2)}) async-start(), calls=%async_computation.16 | async-start | bytes 2949120 | tf_op jit(solution)/shard_map/reduce_scatter | solution.py:226
  388.6 54.0 %copy-start.3 = (bf16[1,1024,4,72]{1,3,2,0:T(8,128)(2,1)S(1)}, bf16[1,1024,4,72]{1,3,2,0:T(8,128)(2,1)}, u32[]{:S(2)}) copy-start(bf16[1,1024,4,72]{1,3,2,0:T(8,128)(2,1)} %get-tuple-element.481) | copy-start | bytes 1769476
  388.6 54.0 %copy-start.7 = (bf16[1,1024,4,72]{1,3,2,0:T(8,128)(2,1)S(1)}, bf16[1,1024,4,72]{1,3,2,0:T(8,128)(2,1)}, u32[]{:S(2)}) copy-start(bf16[1,1024,4,72]{1,3,2,0:T(8,128)(2,1)} %get-tuple-element.482) | copy-start | bytes 1769476
  447.2 2.3 copy-start.9
  449.4 2.9 copy-start.5
  452.4 2.1 copy-start.15
  461.5 2.3 copy-start.9
  463.8 2.9 copy-start.5
  466.8 2.1 copy-start.15
  471.3 2.2 copy-start.6
  471.4 3.8 copy-start.18
  471.4 2.2 copy-start.25
  479.7 146.3 %reduce-scatter.28.cloned.1.call-start = ((), (), s32[]{:S(2)}) async-start(), calls=%async_computation.22 | async-start | bytes 4644864
  480.0 2.8 copy-start.51
  504.5 1.7 copy-start.53
  504.6 137.5 %reduce-scatter.26.cloned.1.call-start = ((), (), s32[]{:S(2)}) async-start(), calls=%async_computation.21 | async-start | bytes 5971968 | tf_op jit(solution)/shard_map/reduce_scatter | solution.py:265
  514.3 1.7 copy-start.52
  514.3 188.6 %reduce-scatter.24.cloned.1.call-start = ((), (), s32[]{:S(2)}) async-start(), calls=%async_computation.20 | async-start | bytes 5971968 | tf_op jit(solution)/shard_map/reduce_scatter | solution.py:264
  523.3 222.7 %reduce-scatter.22.cloned.1.call-start = ((), (), s32[]{:S(2)}) async-start(), calls=%async_computation.19 | async-start | bytes 1990656 | tf_op jit(solution)/shard_map/reduce_scatter | solution.py:263
  524.3 4.8 copy-start.29
  524.3 4.8 copy-start.42
  524.3 4.8 copy-start.44
  528.7 2.1 copy-start.39
  528.7 2.2 copy-start.38
  528.7 367.2 %all-reduce.7.cloned.1.call-start = ((), (), s32[]{:S(2)}) async-start(), calls=%async_computation.17 | async-start | bytes 9289728 | tf_op jit(solution)/shard_map/psum | solution.py:258
  530.8 17.6 %copy-start.31 = (f32[1152]{0:T(1024)S(1)}, f32[1152]{0:T(1024)}, u32[]{:S(2)}) copy-start(f32[1152]{0:T(1024)} %copy-done.30) | copy-start | bytes 13828
  530.8 17.6 %copy-start.33 = (f32[576]{0:T(1024)S(1)}, f32[576]{0:T(1024)}, u32[]{:S(2)}) copy-start(f32[576]{0:T(1024)} %copy-done.32) | copy-start | bytes 6916
  530.8 17.6 %copy-start.35 = (f32[576]{0:T(1024)S(1)}, f32[576]{0:T(1024)}, u32[]{:S(2)}) copy-start(f32[576]{0:T(1024)} %copy-done.34) | copy-start | bytes 6916
  551.0 420.0 %reduce-scatter.20.cloned.1.call-start = ((), (), s32[]{:S(2)}) async-start(), calls=%async_computation.18 | async-start | bytes 9289728 | tf_op jit(solution)/shard_map/reduce_scatter | solution.py:266
  555.4 2.5 copy-start.37
  555.4 2.6 copy-start.36
  555.4 2.6 copy-start.17
  555.4 45.5 %copy-start.47 = (f32[1152]{0:T(1024)S(1)}, f32[1152]{0:T(1024)}, u32[]{:S(2)}) copy-start(f32[1152]{0:T(1024)} %get-tuple-element.261) | copy-start | bytes 13828
  555.5 69.1 %copy-start.14 = (f32[1,256,1152]{2,1,0:T(8,128)S(1)}, f32[1,256,1152]{2,1,0:T(8,128)}, u32[]{:S(2)}) copy-start(f32[1,256,1152]{2,1,0:T(8,128)} %copy-done.13) | copy-start | bytes 3538948
  555.5 69.1 %copy-start.23 = (bf16[1,256,1152]{2,1,0:T(8,128)(2,1)S(1)}, bf16[1,256,1152]{2,1,0:T(8,128)(2,1)}, u32[]{:S(2)}) copy-start(bf16[1,256,1152]{2,1,0:T(8,128)(2,1)} %reduce-scatter.18.cloned.1.call-done) | copy-start | bytes 1769476
  971.0 4.9 copy-start.1
  (17 other events, 17.4 us)
Sparse Core Ops, SparseCore 0:
  37.3 51.7 all-gather.5
  120.4 46.2 reduce-scatter.11
  171.0 49.5 all-gather.7
  222.6 48.7 all-gather.9
  287.7 46.2 reduce-scatter.15
  336.1 47.0 reduce-scatter.13
  388.4 49.5 all-gather.11
  479.9 46.2 reduce-scatter.17
  529.6 51.4 reduce-scatter.27
  584.9 57.1 reduce-scatter.25
  646.0 56.8 reduce-scatter.23
  706.7 39.2 reduce-scatter.21
  752.2 143.6 all-reduce.6
  900.0 70.8 reduce-scatter.19
where the time goes:
time: 993 us; the launch traced here: 983 us
  waiting for transfers between devices  665 us (67%)
  matrix products  109 us (11%)
  blocking collectives  94.6 us (10%)
  local copies, waits for them, and re-layouts  47.5 us (5%)
  other arithmetic  39 us (4%)
  between operations  18.5 us (2%)
    psum x1, waiting for transfers between devices, body(): lax.psum((table_part, out_bias_part, qv_full), ('dp', 'tensor'))  150 us
    reduce_scatter x1, waiting for transfers between devices, body(): lax.psum_scatter(ada_grad, 'dp', scatter_dimension=0, tiled=True)  75 us
    reduce_scatter x1, waiting for transfers between devices, body(): lax.psum_scatter(fc1_grad, 'dp', scatter_dimension=0, tiled=True)  60.9 us
    all_gather x1, waiting for transfers between devices, body(): attn_rows = lax.all_gather(attn_input, 'tensor', axis=1, tiled=True)  51.9 us
    all_gather x1, waiting for transfers between devices, body(): lax.all_gather(attn_grad.astype(jnp.bfloat16), 'tensor', axis=1, tiled=True)  49.5 us
    all_gather x1, waiting for transfers between devices, body(): mlp_rows = lax.all_gather(mlp_input, 'tensor', axis=1, tiled=True)  47.2 us
    reduce_scatter x1, waiting for transfers between devices, body(): lax.psum_scatter(mlp_terms.astype(jnp.bfloat16), 'tensor', scatter_dimens...  46.9 us
    reduce_scatter x1, waiting for transfers between devices, body(): lax.psum_scatter(attn_terms.astype(jnp.bfloat16), 'tensor', scatter_dimen...  46.3 us
  transfers between devices with their start and end apart: 14, of which 12 were waited for; matrix products, arithmetic and copies ran while one was open for 8% of the time, Pallas kernels for 0%

commit v1 on v0

--- a/solution.py
+++ b/solution.py
@@ -240,32 +240,42 @@
         ],
         axis=1,
     )
-    mod_grad = lax.psum(mod_part_grad, "tensor")
     col_count = ada_weight.shape[1]
-    mod_cols = lax.dynamic_slice_in_dim(mod_grad, tensor_rank * col_count, col_count, 1)
-    ada_grad = jnp.dot(cond_low.astype(jnp.float32).T, mod_cols, precision=highest)
-    ada_bias_grad = jnp.sum(mod_cols, axis=0)
-    silu_grad = jnp.dot(mod_cols, ada_weight.astype(jnp.float32).T, precision=highest)
-    unused_cond, silu_pull = jax.vjp(jax.nn.silu, cond)
-    cond_part = silu_pull(silu_grad)[0]
+    mod_grad = lax.psum_scatter(mod_part_grad, "tensor", scatter_dimension=1, tiled=True)
+    small = jnp.concatenate([mod_grad, cond, labels.astype(jnp.float32)[:, None]], axis=1)
+    every = lax.all_gather(small, "dp", axis=0, tiled=True)
+    mod_all, cond_all, label_all = (
+        every[:, :col_count],
+        every[:, col_count : col_count + width],
+        every[:, col_count + width].astype(jnp.int32),
+    )
+    low_all = jax.nn.silu(cond_all).astype(jnp.bfloat16).astype(jnp.float32)
+    dp_rank, dp_size = lax.axis_index("dp"), lax.axis_size("dp")
+    row_count = width // dp_size
+    low_rows = lax.dynamic_slice_in_dim(low_all, dp_rank * row_count, row_count, 1)
+    ada_part = jnp.dot(low_rows.T, mod_all, precision=highest)
+    bias_count = col_count // dp_size
+    ada_bias_part = lax.dynamic_slice_in_dim(
+        jnp.sum(mod_all, axis=0), dp_rank * bias_count, bias_count, 0
+    )
+    silu_terms = jnp.dot(mod_all, ada_weight.astype(jnp.float32).T, precision=highest)
     qv_full = lax.dynamic_update_slice_in_dim(
         jnp.zeros((2, width), jnp.float32), qv_local, tensor_rank * head_cols, 1
     )
     out_bias_part = jnp.stack([attn_bias_grad, mlp_bias_grad])
+    silu_grad = lax.psum(silu_terms, "tensor")
+    out_bias_grad, qv_bias_grad = lax.psum((out_bias_part, qv_full), ("dp", "tensor"))
+    unused_cond, silu_pull = jax.vjp(jax.nn.silu, cond_all)
+    cond_grad = silu_pull(silu_grad)[0]
     class_ids = jnp.arange(label_table.shape[0], dtype=jnp.int32)
-    one_hot = (labels[:, None] == class_ids[None, :]).astype(jnp.float32)
-    table_part = jnp.dot(one_hot.T, cond_part, precision=highest)
-    table_grad, out_bias_grad, qv_bias_grad = lax.psum(
-        (table_part, out_bias_part, qv_full), ("dp", "tensor")
-    )
-    qkv_part, proj_part, fc1_part, fc2_part, ada_part, fc1_bias_part, ada_bias_part = (
+    one_hot = (label_all[:, None] == class_ids[None, :]).astype(jnp.float32)
+    table_grad = jnp.dot(one_hot.T, cond_grad, precision=highest)
+    qkv_part, proj_part, fc1_part, fc2_part, fc1_bias_part = (
         lax.psum_scatter(qkv_grad, "dp", scatter_dimension=1, tiled=True),
         lax.psum_scatter(proj_grad, "dp", scatter_dimension=1, tiled=True),
         lax.psum_scatter(fc1_grad, "dp", scatter_dimension=0, tiled=True),
         lax.psum_scatter(fc2_grad, "dp", scatter_dimension=1, tiled=True),
-        lax.psum_scatter(ada_grad, "dp", scatter_dimension=0, tiled=True),
         lax.psum_scatter(fc1_bias_grad, "dp", scatter_dimension=0, tiled=True),
-        lax.psum_scatter(ada_bias_grad, "dp", scatter_dimension=0, tiled=True),
     )
     return (
         output,

time: 993 us -> 833 us (0.84)
  waiting for transfers between devices: 665 us -> 503 us
    psum x1 -> x0, waiting for transfers between devices: 150 us -> none  [body(): lax.psum((table_part, out_bias_part, qv_full), ('dp', 'tensor'))]
    reduce_scatter x1 -> x0, waiting for transfers between devices: 75 us -> none  [body(): lax.psum_scatter(ada_grad, 'dp', scatter_dimension=0, tiled=True)]
    reduce_scatter x1, waiting for transfers between devices: 0.02 us -> 39.3 us  [body(): lax.psum_scatter(attn_back_terms.astype(jnp.bfloat16), 'tensor', scatter_...]
    reduce_scatter x1, waiting for transfers between devices: 13.4 us -> 36.2 us  [body(): lax.psum_scatter(fc2_grad, 'dp', scatter_dimension=1, tiled=True)]
    all_gather x0 -> x1, blocking collectives: none -> 10.6 us  [body(): every = lax.all_gather(small, 'dp', axis=0, tiled=True)]
    unnamed x115 -> x96, local copies, waits for them, and re-layouts: 37.3 us -> 35.4 us
  transfers between devices with their start and end apart: 14 -> 13, of which waited for: 12 -> 11; matrix products, arithmetic and copies ran while one was open for 8% -> 11% of each run, Pallas kernels for 0% -> 0%
where the time goes in v1:
time: 833 us; the launch traced here: 823 us
  waiting for transfers between devices  503 us (60%)
  matrix products  118 us (14%)
  blocking collectives  96.7 us (12%)
  local copies, waits for them, and re-layouts  46.1 us (6%)
  other arithmetic  33.4 us (4%)
  between operations  17.7 us (2%)
    reduce_scatter x1, waiting for transfers between devices, body(): lax.psum_scatter(fc1_grad, 'dp', scatter_dimension=0, tiled=True)  60.7 us
    all_gather x1, waiting for transfers between devices, body(): attn_rows = lax.all_gather(attn_input, 'tensor', axis=1, tiled=True)  51.9 us
    all_gather x1, waiting for transfers between devices, body(): lax.all_gather(attn_grad.astype(jnp.bfloat16), 'tensor', axis=1, tiled=True)  49.5 us
    reduce_scatter x1, waiting for transfers between devices, body(): lax.psum_scatter(mlp_terms.astype(jnp.bfloat16), 'tensor', scatter_dimens...  47.5 us
    all_gather x1, waiting for transfers between devices, body(): mlp_rows = lax.all_gather(mlp_input, 'tensor', axis=1, tiled=True)  47.2 us
    reduce_scatter x1, waiting for transfers between devices, body(): lax.psum_scatter(attn_terms.astype(jnp.bfloat16), 'tensor', scatter_dimen...  46.3 us
    reduce_scatter x1, waiting for transfers between devices, body(): lax.psum_scatter(proj_grad, 'dp', scatter_dimension=1, tiled=True)  43.2 us
    all_gather x1, waiting for transfers between devices, body(): lax.all_gather(mlp_grad.astype(jnp.bfloat16), 'tensor', axis=1, tiled=True)  42.6 us
  transfers between devices with their start and end apart: 13, of which 11 were waited for; matrix products, arithmetic and copies ran while one was open for 11% of the time, Pallas kernels for 0%

profile of v1, /device:TPU:1, one launch (start us, length us, event | category | flops | bytes accessed | tf_op | source)
XLA Modules:
  0.0 822.7 jit_solution(3532911890009437417)
XLA Ops:
  14.9 3.3 convolution_reduce_fusion
  18.4 16.4 %all-reduce = f32[6912]{0:T(1024)S(1)} all-reduce(f32[6912]{0:T(1024)S(1)} %add_dynamic-update-slice_fusion), channel_id=2, replica_groups=mesh['dp'=8,'tensor'=4] {'tensor'}, use_global_device_ids=true, to_apply=%add | all-reduce | flops 6912 | bytes 55296
  36.7 51.9 %all-gather.7.cloned.1.call-done = bf16[1,1024,1152]{2,1,0:T(8,128)(2,1)} async-done(((bf16[1,256,1152]{2,1,0:T(8,128)(2,1)}), bf16[1,1024,1152]{2,1,0:T(8,128)(2,1)}) %all-gather.7.cloned.1.call-update) | async-done | bytes 2359312 | tf_op jit(solution)/shard_map/all_gather | solution.py:68
  88.5 3.7 fusion.104
  92.3 1.8 fusion.98
  94.0 1.8 fusion.101
  96.7 17.3 %while.28 = (s32[]{:T(128)}, bf16[2,1,512,4,72]{2,4,3,1,0:T(8,128)(2,1)}, f32[2,1,4,512]{3,2,1,0:T(4,128)S(1)}, s32[2]{0:T(128)S(1)}, bf16[1,1024,4,72]{1,3,2,0:...) while((s32[]{:T(128)}, ...), condition=%wide.region_5.6_spmd, body=%wide.region_2.5_spmd.sunk | while | flops 622999552 | bytes 34078988 | solution.py:104
  97.9 2.6 multiply_reduce_fusion.7
  100.5 1.8 fusion.197
  102.3 2.2 fusion.198
  106.6 2.6 multiply_reduce_fusion.7
  109.2 1.8 fusion.197
  111.0 2.2 fusion.198
  114.0 1.7 copy.30
  116.7 2.9 fusion.54
  119.7 46.3 %reduce-scatter.14.cloned.1.call-done = bf16[1,256,1152]{2,1,0:T(8,128)(2,1)} async-done(((bf16[1,1024,1152]{2,1,0:T(8,128)(2,1)}), bf16[1,256,1152]{2,1,0:T(8,128)(2,1)}) %reduce-scatter.14.cloned.1.call-update) | async-done | bytes 589840 | tf_op jit(solution)/shard_map/reduce_scatter | solution.py:110
  170.3 2.0 fusion.91
  172.8 47.2 %all-gather.9.cloned.1.call-done = bf16[1,1024,1152]{2,1,0:T(8,128)(2,1)} async-done(((bf16[1,256,1152]{2,1,0:T(8,128)(2,1)}), bf16[1,1024,1152]{2,1,0:T(8,128)(2,1)}) %all-gather.9.cloned.1.call-update) | async-done | bytes 2359312 | tf_op jit(solution)/shard_map/all_gather | solution.py:118
  220.0 8.2 convolution_add_fusion.2
  228.2 42.6 %all-gather.11.cloned.1.call-done = bf16[1,1024,1152]{2,1,0:T(8,128)(2,1)} async-done(((bf16[1,256,1152]{2,1,0:T(8,128)(2,1)}), bf16[1,1024,1152]{2,1,0:T(8,128)(2,1)}) %all-gather.11.cloned.1.call-update) | async-done | bytes 2359312 | tf_op jit(solution)/shard_map/all_gather | solution.py:136
  270.8 9.9 %convert_reduce_fusion = (f32[1152]{0:T(1024)}, bf16[1024,1152]{1,0:T(8,128)(2,1)S(1)}) fusion(f32[1024,1152]{1,0:T(8,128)} %convolution_add_fusion.2, bf16[1152,1152]{1,0:T(8,128)(2,1)S(1)} %copy-done, bf16[1,1024,1152]{2,1,0:T(8,128)(2,1)} %all-gather.11.cloned.1.call-done), kind=kOutput, calls=%fused_computation.62 | convolution fusion | flops 2743860224 | bytes 12096000 | tf_op jit(solution)/shard_map/lsd,cd->lsc/dot_general | solution.py:137
  282.1 4.8 fusion.57
  287.0 7.9 fusion.56
  295.0 38.3 %reduce-scatter.18.cloned.1.call-done = bf16[1,256,1152]{2,1,0:T(8,128)(2,1)} async-done(((bf16[1,1024,1152]{2,1,0:T(8,128)(2,1)}), bf16[1,256,1152]{2,1,0:T(8,128)(2,1)}) %reduce-scatter.18.cloned.1.call-update) | async-done | bytes 589840 | tf_op jit(solution)/shard_map/reduce_scatter | solution.py:148
  333.3 1.8 fusion.121
  335.1 47.5 %reduce-scatter.16.cloned.1.call-done = bf16[1,256,1152]{2,1,0:T(8,128)(2,1)} async-done(((bf16[1,1024,1152]{2,1,0:T(8,128)(2,1)}), bf16[1,256,1152]{2,1,0:T(8,128)(2,1)}) %reduce-scatter.16.cloned.1.call-update) | async-done | bytes 589840 | tf_op jit(solution)/shard_map/reduce_scatter | solution.py:126
  382.6 3.5 multiply_reduce_fusion.4
  387.4 49.5 %all-gather.13.cloned.1.call-done = bf16[1,1024,1152]{2,1,0:T(8,128)(2,1)} async-done(((bf16[1,256,1152]{2,1,0:T(8,128)(2,1)}), bf16[1,1024,1152]{2,1,0:T(8,128)(2,1)}) %all-gather.13.cloned.1.call-update) | async-done | bytes 2359312 | tf_op jit(solution)/shard_map/all_gather | solution.py:157
  436.8 3.6 fusion.107
  441.3 28.8 %while.29 = (s32[]{:T(128)}, f32[1,1024,4,72]{1,3,2,0:T(8,128)S(1)}, f32[1,1024,4,72]{1,3,2,0:T(8,128)}, bf16[2,1,512,4,72]{2,4,3,1,0:T(8,128)(2,1)}, s32[2]{0:T...) while((s32[]{:T(128)}, ...), condition=%wide.region_15.16_spmd.clone, body=%wide.region_13.15_spmd.clone.sunk | while | flops 1536882688 | bytes 89809336 | solution.py:203
  445.9 2.3 fusion.209
  448.2 2.9 multiply_reduce_fusion.8
  451.1 2.1 multiply_convert_fusion.7
  460.3 2.3 fusion.209
  462.6 2.9 multiply_reduce_fusion.8
  465.5 2.1 multiply_convert_fusion.7
  470.2 1.9 copy.31
  475.5 3.0 fusion.55
  478.8 2.7 convolution_bitcast_fusion
  481.6 2.0 convolution_bitcast_fusion.2
  483.6 2.1 convolution_bitcast_fusion.1
  485.6 39.3 %reduce-scatter.20.cloned.1.call-done = bf16[1,256,1152]{2,1,0:T(8,128)(2,1)} async-done(((bf16[1,1024,1152]{2,1,0:T(8,128)(2,1)}), bf16[1,256,1152]{2,1,0:T(8,128)(2,1)}) %reduce-scatter.20.cloned.1.call-update) | async-done | bytes 589840 | tf_op jit(solution)/shard_map/reduce_scatter | solution.py:226
  524.9 1.7 fusion.122
  526.7 2.4 copy.33
  529.2 3.9 pad_maximum_fusion
  533.1 8.6 %copy.35 = f32[3,1152,288]{2,0,1:T(4,128)} copy(f32[3,1152,288]{1,2,0:T(8,128)} %pad_maximum_fusion) | data formatting | bytes 7962624
  541.7 8.9 %reshape.501 = f32[1152,864]{1,0:T(8,128)} reshape(f32[1152,3,288]{2,1,0:T(4,128)} %bitcast.239) | data formatting | bytes 7962624
  550.7 1.6 copy-done.43
  552.3 8.0 fusion.62
  560.4 1.6 copy-done.42
  562.0 7.3 fusion.68
  571.2 13.4 %all-reduce.1 = f32[1152]{0:T(1024)S(1)} all-reduce(f32[1152]{0:T(1024)S(1)} %copy-done.37), channel_id=11, replica_groups=mesh['dp'=8,'tensor'=4] {'dp'}, use_global_device_ids=true, to_apply=%region_38.39.clone | all-reduce | flops 1152 | bytes 9216
  585.7 4.4 fusion.58
  590.4 42.1 %all-reduce.2 = (f32[2,1152]{1,0:T(2,128)}, f32[2,1152]{1,0:T(2,128)}) all-reduce(f32[2,1152]{1,0:T(2,128)S(1)} %dynamic_update_slice.14, f32[2,1152]{1,0:T(2,128)S(1)} %pad_maximum_fusion.1), channel_id=1, replica_groups=mesh['dp'=8,'tensor'=4] {'dp','tensor'}, use_global_device_ids=true, to_apply=%region_31.32 | all-reduce | flops 4608 | bytes 36864 | tf_op jit(solution)/shard_map/psum | solution.py:267
  635.5 10.6 %all-gather.1 = f32[8,1,2881]{2,1,0:T(1,128)S(1)} all-gather(f32[1,1,2881]{2,1,0:T(1,128)S(1)} %bitcast.261), channel_id=1, replica_groups=mesh['dp'=8,'tensor'=4] {'dp'}, dimensions={0}, use_global_device_ids=true | all-gather | bytes 103716 | tf_op jit(solution)/shard_map/all_gather | solution.py:246
  646.7 3.8 fusion.138
  650.6 14.3 %psum.21 = f32[8,1152]{1,0:T(8,128)S(1)} all-reduce(f32[8,1152]{1,0:T(8,128)S(1)} %fusion.138), channel_id=1, replica_groups=mesh['dp'=8,'tensor'=4] {'tensor'}, use_global_device_ids=true, to_apply=%region_26.27 | all-reduce | flops 9216 | bytes 73728 | tf_op jit(solution)/shard_map/psum | solution.py:266
  665.1 1.6 fusion.136
  666.8 4.3 fusion.142
  671.1 2.4 reshape.502
  673.5 2.0 copy.32
  675.5 36.2 %reduce-scatter.26.cloned.1.call-done = f32[1152,144]{0,1:T(8,128)} async-done(((f32[1152,1152]{0,1:T(8,128)}), f32[1152,144]{0,1:T(8,128)}) %reduce-scatter.26.cloned.1.call-update) | async-done | bytes 663568 | tf_op jit(solution)/shard_map/reduce_scatter | solution.py:277
  711.8 60.7 %reduce-scatter.24.cloned.1.call-done = f32[144,1152]{1,0:T(8,128)} async-done(((f32[1152,1152]{1,0:T(8,128)}), f32[144,1152]{1,0:T(8,128)}) %reduce-scatter.24.cloned.1.call-update) | async-done | bytes 663568 | tf_op jit(solution)/shard_map/reduce_scatter | solution.py:276
  772.5 43.2 %reduce-scatter.22.cloned.1.call-done = f32[288,144]{0,1:T(8,128)} async-done(((f32[288,1152]{0,1:T(8,128)}), f32[288,144]{0,1:T(8,128)}) %reduce-scatter.22.cloned.1.call-update) | async-done | bytes 165904 | tf_op jit(solution)/shard_map/reduce_scatter | solution.py:275
  (220 shorter events, 39.9 us)
Async XLA Ops:
  7.2 263.6 %copy-start = (bf16[1152,1152]{1,0:T(8,128)(2,1)S(1)}, bf16[1152,1152]{1,0:T(8,128)(2,1)}, u32[]{:S(2)}) copy-start(bf16[1152,1152]{1,0:T(8,128)(2,1)} %param.30) | copy-start | bytes 7962628
  7.2 81.3 %all-gather.7.cloned.1.call-start = ((), (), s32[]{:S(2)}) async-start(), calls=%async_computation.9 | async-start | bytes 2949120 | tf_op jit(solution)/shard_map/all_gather | solution.py:68
  9.9 8.3 %copy-start.36 = (f32[1728]{0:T(1024)S(1)}, f32[1728]{0:T(1024)}, u32[]{:S(2)}) copy-start(f32[1728]{0:T(1024)} %param.23) | copy-start | bytes 20740
  9.9 24.9 %copy-start.30 = (f32[256]{0:T(256)}, f32[256]{0:T(256)S(1)}, u32[]{:S(2)}) copy-start(f32[256]{0:T(256)S(1)} %broadcast_multiply_fusion.5) | copy-start | bytes 3076
  9.9 25.5 %copy-start.2 = (bf16[1,256,1152]{2,1,0:T(8,128)(2,1)S(1)}, bf16[1,256,1152]{2,1,0:T(8,128)(2,1)}, u32[]{:S(2)}) copy-start(bf16[1,256,1152]{2,1,0:T(8,128)(2,1)} %param.18) | copy-start | bytes 1769476
  11.4 25.2 %copy-start.33 = (f32[256]{0:T(256)}, f32[256]{0:T(256)S(1)}, u32[]{:S(2)}) copy-start(f32[256]{0:T(256)S(1)} %add_rsqrt_fusion.1) | copy-start | bytes 3076
  14.9 21.7 %copy-start.38 = (f32[2,288]{1,0:T(2,128)S(1)}, f32[2,288]{1,0:T(2,128)}, u32[]{:S(2)}) copy-start(f32[2,288]{1,0:T(2,128)} %param.25) | copy-start | bytes 6916
  36.6 129.5 %reduce-scatter.14.cloned.1.call-start = ((), (), s32[]{:S(2)}) async-start(), calls=%async_computation.10 | async-start | bytes 2949120 | tf_op jit(solution)/shard_map/reduce_scatter | solution.py:110
  88.5 3.7 copy-start.24
  88.5 3.7 copy-start.40
  100.5 1.8 copy-start.8
  100.5 1.8 copy-start.20
  109.1 1.8 copy-start.8
  109.1 1.8 copy-start.20
  114.0 2.7 copy-start.44
  116.7 3.0 copy-start.35
  119.6 100.4 %all-gather.9.cloned.1.call-start = ((), (), s32[]{:S(2)}) async-start(), calls=%async_computation.11 | async-start | bytes 2949120 | tf_op jit(solution)/shard_map/all_gather | solution.py:118
  166.1 2.9 copy-start.10
  169.0 51.0 %copy-start.45 = (f32[1152]{0:T(1024)S(1)}, f32[1152]{0:T(1024)}, u32[]{:S(2)}) copy-start(f32[1152]{0:T(1024)} %param.29) | copy-start | bytes 13828
  170.3 100.5 %all-gather.11.cloned.1.call-start = ((), (), s32[]{:S(2)}) async-start(), calls=%async_computation.13 | async-start | bytes 2949120 | tf_op jit(solution)/shard_map/all_gather | solution.py:136
  172.3 161.0 %reduce-scatter.18.cloned.1.call-start = ((), (), s32[]{:S(2)}) async-start(), calls=%async_computation.14 | async-start | bytes 2949120 | tf_op jit(solution)/shard_map/reduce_scatter | solution.py:148
  270.8 11.4 %copy-start.39 = (bf16[1152,1152]{1,0:T(8,128)(2,1)S(1)}, bf16[1152,1152]{1,0:T(8,128)(2,1)}, u32[]{:S(2)}) copy-start(bf16[1152,1152]{1,0:T(8,128)(2,1)} %param.28) | copy-start | bytes 7962628
  280.7 1.4 copy-start.47
  286.9 95.7 %reduce-scatter.16.cloned.1.call-start = ((), (), s32[]{:S(2)}) async-start(), calls=%async_computation.12 | async-start | bytes 2949120 | tf_op jit(solution)/shard_map/reduce_scatter | solution.py:126
  294.9 38.4 %copy-start.11 = (bf16[1,256,1152]{2,1,0:T(8,128)(2,1)S(1)}, bf16[1,256,1152]{2,1,0:T(8,128)(2,1)}, u32[]{:S(2)}) copy-start(bf16[1,256,1152]{2,1,0:T(8,128)(2,1)} %reduce-scatter.14.cloned.1.call-done) | copy-start | bytes 1769476
  294.9 87.7 %copy-start.22 = (bf16[1,256,1152]{2,1,0:T(8,128)(2,1)S(1)}, bf16[1,256,1152]{2,1,0:T(8,128)(2,1)}, u32[]{:S(2)}) copy-start(bf16[1,256,1152]{2,1,0:T(8,128)(2,1)} %param.31) | copy-start | bytes 1769476
  294.9 141.9 %all-gather.13.cloned.1.call-start = ((), (), s32[]{:S(2)}) async-start(), calls=%async_computation.15 | async-start | bytes 2949120 | tf_op jit(solution)/shard_map/all_gather | solution.py:157
  386.1 1.2 copy-start.13
  387.1 137.9 %reduce-scatter.20.cloned.1.call-start = ((), (), s32[]{:S(2)}) async-start(), calls=%async_computation.16 | async-start | bytes 2949120 | tf_op jit(solution)/shard_map/reduce_scatter | solution.py:226
  387.3 54.0 %copy-start.3 = (bf16[1,1024,4,72]{1,3,2,0:T(8,128)(2,1)S(1)}, bf16[1,1024,4,72]{1,3,2,0:T(8,128)(2,1)}, u32[]{:S(2)}) copy-start(bf16[1,1024,4,72]{1,3,2,0:T(8,128)(2,1)} %get-tuple-element.468) | copy-start | bytes 1769476
  387.3 54.0 %copy-start.7 = (bf16[1,1024,4,72]{1,3,2,0:T(8,128)(2,1)S(1)}, bf16[1,1024,4,72]{1,3,2,0:T(8,128)(2,1)}, u32[]{:S(2)}) copy-start(bf16[1,1024,4,72]{1,3,2,0:T(8,128)(2,1)} %get-tuple-element.469) | copy-start | bytes 1769476
  444.5 1.3 copy-start.4
  444.5 1.4 copy-start.12
  445.9 2.3 copy-start.9
  448.2 2.9 copy-start.5
  451.1 2.1 copy-start.15
  454.6 1.0 copy-start.16
  458.9 1.3 copy-start.4
  458.9 1.4 copy-start.12
  460.3 2.3 copy-start.9
  462.6 2.9 copy-start.5
  465.5 2.1 copy-start.15
  470.1 2.2 copy-start.6
  470.2 3.8 copy-start.18
  470.2 2.2 copy-start.25
  478.5 155.4 %reduce-scatter.28.cloned.1.call-start = ((), (), s32[]{:S(2)}) async-start(), calls=%async_computation.20 | async-start | bytes 4423680
  478.8 2.8 copy-start.41
  481.6 2.0 copy-start.19
  483.6 41.4 %copy-start.29 = (f32[1152]{0:T(1024)S(1)}, f32[1152]{0:T(1024)}, u32[]{:S(2)}) copy-start(f32[1152]{0:T(1024)} %copy-done.28) | copy-start | bytes 13828
  483.6 41.4 %copy-start.31 = (f32[256]{0:T(256)S(1)}, f32[256]{0:T(256)}, u32[]{:S(2)}) copy-start(f32[256]{0:T(256)} %copy-done.30) | copy-start | bytes 3076
  483.6 41.4 %copy-start.34 = (f32[256]{0:T(256)S(1)}, f32[256]{0:T(256)}, u32[]{:S(2)}) copy-start(f32[256]{0:T(256)} %copy-done.33) | copy-start | bytes 3076
  529.1 141.9 %reduce-scatter.30.cloned.1.call-start = ((), (), s32[]{:S(2)}) async-start(), calls=%async_computation.21 | async-start | bytes 4644864
  550.7 1.7 copy-start.43
  550.7 161.1 %reduce-scatter.26.cloned.1.call-start = ((), (), s32[]{:S(2)}) async-start(), calls=%async_computation.19 | async-start | bytes 5971968 | tf_op jit(solution)/shard_map/reduce_scatter | solution.py:277
  560.3 1.7 copy-start.42
  560.4 212.1 %reduce-scatter.24.cloned.1.call-start = ((), (), s32[]{:S(2)}) async-start(), calls=%async_computation.18 | async-start | bytes 5971968 | tf_op jit(solution)/shard_map/reduce_scatter | solution.py:276
  569.3 1.9 copy-start.37
  569.3 16.0 %copy-start.17 = (bf16[2,1,512,4,72]{2,4,3,1,0:T(8,128)(2,1)S(1)}, bf16[2,1,512,4,72]{2,4,3,1,0:T(8,128)(2,1)}, u32[]{:S(2)}) copy-start(bf16[2,1,512,4,72]{2,4,3,1,0:T(8,128)(2,1)} %get-tuple-element.106) | copy-start | bytes 1769476
  569.3 16.4 %copy-start.27 = (bf16[36,8,2,512]{3,1,2,0:T(8,128)(2,1)S(1)}, bf16[36,8,2,512]{3,1,2,0:T(8,128)(2,1)}, u32[]{:S(2)}) copy-start(bf16[36,8,2,512]{3,1,2,0:T(8,128)(2,1)} %copy-done.26) | copy-start | bytes 1769476
  569.3 246.4 %reduce-scatter.22.cloned.1.call-start = ((), (), s32[]{:S(2)}) async-start(), calls=%async_computation.17 | async-start | bytes 1990656 | tf_op jit(solution)/shard_map/reduce_scatter | solution.py:275
  585.7 46.8 %copy-start.23 = (bf16[1,256,1152]{2,1,0:T(8,128)(2,1)S(1)}, bf16[1,256,1152]{2,1,0:T(8,128)(2,1)}, u32[]{:S(2)}) copy-start(bf16[1,256,1152]{2,1,0:T(8,128)(2,1)} %reduce-scatter.20.cloned.1.call-done) | copy-start | bytes 1769476
  590.1 42.3 %copy-start.14 = (f32[1,256,1152]{2,1,0:T(8,128)S(1)}, f32[1,256,1152]{2,1,0:T(8,128)}, u32[]{:S(2)}) copy-start(f32[1,256,1152]{2,1,0:T(8,128)} %copy-done.13) | copy-start | bytes 3538948
  590.1 45.2 %copy-start.32 = (f32[1,1152]{1,0:T(1,128)S(1)}, f32[1,1152]{1,0:T(1,128)}, u32[]{:S(2)}) copy-start(f32[1,1152]{1,0:T(1,128)} %get-tuple-element.254) | copy-start | bytes 13828
  666.8 149.0 %copy-start.1 = (bf16[1152,1152]{1,0:T(8,128)(2,1)S(1)}, bf16[1152,1152]{1,0:T(8,128)(2,1)}, u32[]{:S(2)}) copy-start(bf16[1152,1152]{1,0:T(8,128)(2,1)} %param.30) | copy-start | bytes 7962628
  (6 other events, 4.8 us)
Sparse Core Ops, SparseCore 0:
  36.7 51.7 all-gather.6
  119.8 46.2 reduce-scatter.13
  170.4 49.5 all-gather.8
  222.0 48.7 all-gather.10
  287.1 46.2 reduce-scatter.17
  335.5 47.0 reduce-scatter.15
  387.2 49.5 all-gather.12
  478.7 46.2 reduce-scatter.19
  529.3 66.3 reduce-scatter.27
  599.0 52.1 reduce-scatter.29
  655.2 56.5 reduce-scatter.25
  715.6 56.8 reduce-scatter.23
  776.5 39.2 reduce-scatter.21

commit v2 on v1

--- a/solution.py
+++ b/solution.py
@@ -3,6 +3,8 @@
 import jax
 import jax.numpy as jnp
 from jax import lax
+from jax.experimental import pallas as pl
+from jax.experimental.pallas import tpu as pltpu
 from jax.sharding import PartitionSpec as P
 
 HEAD_DIM = 72
@@ -293,6 +295,940 @@
     )
 
 
+MESH = pl.DeviceIdType.MESH
+f32, bf16 = jnp.float32, jnp.bfloat16
+LANES = 128
+
+
+def dot(a, b, dims):
+    return lax.dot_general(a, b, (dims, ((), ())), preferred_element_type=f32)
+
+
+NN, NT, TN = ((1,), (0,)), ((1,), (1,)), ((0,), (0,))
+
+
+class Spot:
+    def __init__(self):
+        self.dp, self.z = lax.axis_index("dp"), lax.axis_index("tensor")
+        self.q, self.p, self.g = self.dp % 2, self.z % 2, self.z // 2
+        self.c = (self.dp // 2) % 4
+        self.rank = self.p + 2 * self.q
+        self.home = self.q == self.g
+        self.away = self.q != self.g
+        self.sib = (self.flip(self.dp, 1), self.z)
+        self.nbr = (self.dp, self.flip(self.z, 1))
+        self.swap = (self.flip(self.dp, 1), self.flip(self.z, 2))
+        self.peers = [(self.flip(self.dp, 2 * k), self.z) for k in (1, 2, 3)]
+        self.r_sib, self.r_nbr, self.r_diag = (self.flip(self.rank, k) for k in (2, 1, 3))
+
+    @staticmethod
+    def flip(value, bits):
+        return jnp.bitwise_xor(value, bits)
+
+
+def send(src, dst, sems, i, dev):
+    return pltpu.make_async_remote_copy(
+        src_ref=src, dst_ref=dst, send_sem=sems.at[0, i], recv_sem=sems.at[1, i],
+        device_id=dev, device_id_type=MESH,
+    )
+
+
+def quarter(rank, size=256):
+    return pl.ds(pl.multiple_of(rank * size, size), size)
+
+
+def loop(count, fn):
+    def step(i, carry):
+        fn(i)
+        return carry
+    lax.fori_loop(0, count, step, 0)
+
+
+class Gather:
+    def __init__(self, at, rows, sems, base):
+        self.at, self.rows, self.sems, self.base = at, rows, sems, base
+
+    def copy(self, rank, i, dev):
+        block = self.rows.at[quarter(rank)]
+        return send(block, block, self.sems, self.base + i, dev)
+
+    def start(self):
+        self.copy(self.at.rank, 0, self.at.nbr).start()
+        self.copy(self.at.rank, 1, self.at.sib).start()
+
+    def take_sib(self):
+        self.copy(self.at.r_sib, 1, self.at.sib).wait_recv()
+
+    def take_nbr(self):
+        self.copy(self.at.r_nbr, 0, self.at.nbr).wait_recv()
+        self.copy(self.at.r_nbr, 2, self.at.sib).start()
+
+    def take_diag(self):
+        self.copy(self.at.r_diag, 2, self.at.sib).wait_recv()
+
+    def finish(self):
+        self.copy(self.at.rank, 0, self.at.nbr).wait_send()
+        self.copy(self.at.rank, 1, self.at.sib).wait_send()
+        self.copy(self.at.r_nbr, 2, self.at.sib).wait_send()
+
+
+class Scatter:
+    def __init__(self, at, out, into, sems, base):
+        self.at, self.out, self.into, self.sems, self.base = at, out, into, sems, base
+
+    def copy(self, i):
+        return send(self.out.at[i], self.into.at[i], self.sems, self.base + i,
+                    self.at.nbr if i == 2 else self.at.sib)
+
+    def start(self, i):
+        self.copy(i).start()
+
+    def take(self, i):
+        self.copy(i).wait_recv()
+
+    def finish(self):
+        for i in range(3):
+            self.copy(i).wait_send()
+
+
+def entry(at, extra=()):
+    barrier = pltpu.get_barrier_semaphore()
+    mates = [at.sib, at.nbr, at.swap, *at.peers, *extra]
+    for mate in mates:
+        pl.semaphore_signal(barrier, inc=1, device_id=mate, device_id_type=MESH)
+    pl.semaphore_wait(barrier, len(mates))
+
+
+def center_rows(x):
+    mean = jnp.mean(x, axis=1, keepdims=True)
+    center = x - mean
+    inv = lax.rsqrt(jnp.mean(center * center, axis=1, keepdims=True) + 1e-6)
+    return center * inv, inv
+
+
+def split_heads(acc_ref, store):
+    lane = lax.broadcasted_iota(jnp.int32, (acc_ref.shape[0], LANES), 1)
+    for h in range(4):
+        tile, off = divmod(HEAD_DIM * h, LANES)
+        two = acc_ref[:, tile * LANES:(tile + 2) * LANES] if tile < 2 else acc_ref[:, 128:384]
+        if off:
+            two = pltpu.roll(two, 2 * LANES - off, 1)
+        store(h, jnp.where(lane < HEAD_DIM, two[:, :LANES], 0.0))
+
+
+def join_heads(parts):
+    rows = parts[0].shape[0]
+    zero = jnp.zeros((rows, LANES), parts[0].dtype)
+    tiles = [parts[0], zero, zero]
+    for h in (1, 2, 3):
+        tile, off = divmod(HEAD_DIM * h, LANES)
+        two = pltpu.roll(jnp.concatenate([parts[h], zero], axis=1), off, 1)
+        tiles[tile] = tiles[tile] + two[:, :LANES]
+        if tile + 1 < 3:
+            tiles[tile + 1] = tiles[tile + 1] + two[:, LANES:]
+    return jnp.concatenate(tiles, axis=1)[:, :4 * HEAD_DIM]
+
+
+GELU_A, GELU_B = math.sqrt(2.0 / math.pi), 0.044715
+
+S_X, S_C, S_BIAS, S_MOD, S_AG1, S_AG2, S_AG3, S_AG4, S_RS1, S_RS3, S_RS2, S_W1, S_W2 = (
+    0, 1, 2, 3, 7, 10, 13, 16, 19, 22, 25, 28, 38)
+N_SEMS = 38 + 30
+
+
+def kf(tok, cot, mblk, bblk, obias, wqkv, wproj, wfc1, wfc2,
+       xr, qn, kn, vn, kt, lse, mix, gr, mgrad, xs, cs, mid, mods, stats, mlpown, mlpz, g1, g2, wq, wp,
+       w1, w2, vt, mr, cr, hgrad, hid, pgr, rso, rsi, own, nbrf, rs2o, rs2i, n2, branch, mrecv, bias, acc, mixt, inv2,
+       stage, sems, lsem):
+    at = Spot()
+    me = (at.dp, at.z)
+    inv_root = 1.0 / math.sqrt(HEAD_DIM)
+    entry(at, [(at.dp, at.flip(at.z, 2)), (at.dp, at.flip(at.z, 3)), (at.flip(at.dp, 1), at.flip(at.z, 1)),
+               (at.flip(at.dp, 1), at.flip(at.z, 3))])
+    weights = [(wqkv, wq, 288), (wproj, wp, 72), (wfc1, w1, 288), (wfc2, w2, 288)]
+
+    def piece(i, slot, side):
+        if i < 3:
+            return weights[0][side].at[i, pl.ds(pl.multiple_of(slot * 288, 8), 288), :]
+        if i == 3:
+            return weights[1][side].at[pl.ds(pl.multiple_of(slot * 72, 8), 72), :]
+        ref = weights[3 if i < 7 else 2][side]
+        return ref.at[pl.ds(pl.multiple_of(slot * 288 + (i - 4) % 3 * 96, 8), 96), :]
+
+    def import_first(i):
+        return send(piece(i, at.c, 0), piece(i, at.c, 1), sems, S_W1 + i, at.swap)
+
+    def import_next(i, k, slot):
+        block = piece(i, slot, 1)
+        return send(block, block, sems, S_W2 + 3 * i + k, at.peers[k])
+
+    def import_start(*pieces):
+        @pl.when(at.away)
+        def _():
+            for i in pieces:
+                import_first(i).start()
+
+    def import_hand_on(*pieces):
+        @pl.when(at.away)
+        def _():
+            for i in pieces:
+                import_first(i).wait_recv()
+                for k in range(3):
+                    import_next(i, k, at.c).start()
+
+    def import_wait(j, *pieces):
+        @pl.when(at.away)
+        def _():
+            for i in pieces:
+                for k in range(3):
+                    import_next(i, k, at.flip(at.c, k + 1)).wait_recv()
+
+        @pl.when(at.home)
+        def _():
+            pltpu.make_async_copy(weights[j][0], weights[j][1], lsem.at[j]).wait()
+
+    own_rows = quarter(at.rank)
+    cown = cr.at[own_rows]
+
+    @pl.when(at.away)
+    def _():
+        send(tok, xs, sems, S_X, at.swap).start()
+        send(bblk, bias, sems, S_BIAS, at.swap).start()
+        for i in (0, 1, 2):
+            import_first(i).start()
+
+    @pl.when(at.home)
+    def _():
+        pltpu.make_async_copy(tok, xs, sems.at[1, S_X]).start()
+        pltpu.make_async_copy(bblk, bias, sems.at[1, S_BIAS]).start()
+        pltpu.make_async_copy(cot, cown, sems.at[1, S_C]).start()
+        for i in range(4):
+            pltpu.make_async_copy(weights[i][0], weights[i][1], lsem.at[i]).start()
+
+    def mod_copy(core, pp):
+        dev = (at.dp - at.q + core, 2 * at.q + pp)
+        return dev, send(mblk, mrecv.at[at.z], sems, S_MOD, dev)
+
+    def for_mods(remote, local):
+        for core in range(2):
+            for pp in range(2):
+                mine = (at.q == core) & (at.z == 2 * at.q + pp)
+                dev = (at.dp - at.q + core, 2 * at.q + pp)
+                cp = pltpu.make_async_remote_copy(
+                    src_ref=mblk, dst_ref=mrecv.at[at.z], send_sem=sems.at[0, S_MOD + 2 * core + pp],
+                    recv_sem=sems.at[1, S_MOD + at.z], device_id=dev, device_id_type=MESH)
+
+                @pl.when(jnp.logical_not(mine))
+                def _():
+                    remote(cp)
+
+                if local is not None:
+                    @pl.when(mine)
+                    def _():
+                        local(pltpu.make_async_copy(mblk, mrecv.at[at.z], sems.at[1, S_MOD + at.z]))
+
+    for_mods(lambda cp: cp.start(), lambda cp: cp.start())
+    for k in range(4):
+        pltpu.make_async_copy(mblk, mrecv.at[k], sems.at[1, S_MOD + k]).wait()
+    lane = lax.broadcasted_iota(jnp.int32, (1, 1152), 1)
+    rolled = [pltpu.roll(mrecv[k], 576, 1) for k in range(4)]
+    for j in range(6):
+        (ka, ia), (kb, ib) = divmod(2 * j, 3), divmod(2 * j + 1, 3)
+        mods[j:j + 1, :] = jnp.where(lane < 576, mrecv[ka, ia:ia + 1, :], rolled[kb][ib:ib + 1, :])
+    mods[6:8, :] = mrecv[0, 3:5, :]
+    shift_attn, scale_attn, gate_attn, shift_mlp, scale_mlp, gate_mlp = (pl.ds(j, 1) for j in range(6))
+
+    pltpu.make_async_copy(tok, xs, sems.at[1, S_X]).wait()
+
+    def norm_one(i):
+        rows = pl.ds(pl.multiple_of(i * 32, 32), 32)
+        normed, _ = center_rows(xs[rows, :].astype(f32))
+        target = pl.ds(pl.multiple_of(at.rank * 256 + i * 32, 32), 32)
+        xr[target, :] = (normed * (1.0 + mods[scale_attn, :]) + mods[shift_attn, :]).astype(bf16)
+    loop(8, norm_one)
+    ag1 = Gather(at, xr, sems, S_AG1)
+    ag1.start()
+    pltpu.make_async_copy(bblk, bias, sems.at[1, S_BIAS]).wait()
+    import_start(3)
+
+    @pl.when(at.away)
+    def _():
+        send(cot, cr.at[quarter(at.r_sib)], sems, S_C, at.swap).start()
+    import_start(4, 5, 6)
+    import_hand_on(0, 1, 2)
+    import_wait(0, 0, 1, 2)
+
+    def slot_of(i):
+        return at.flip(at.rank, ((i & 1) << 1) | (i >> 1))
+
+    def qkv_block(i):
+        @pl.when(i == 1)
+        def _():
+            ag1.take_sib()
+
+        @pl.when(i == 2)
+        def _():
+            ag1.take_nbr()
+
+        @pl.when(i == 3)
+        def _():
+            ag1.take_diag()
+        rows = quarter(slot_of(i))
+        x = xr[rows, :]
+        for t, (nat, tra) in enumerate(((qn, None), (kn, kt), (vn, vt))):
+            value = dot(x, wq[t], NN)
+            if t != 1:
+                value = value + bias[(1 if t == 0 else 2):(2 if t == 0 else 3), :288]
+            acc[:, :288] = value
+
+            def store(h, head):
+                nat[h, rows, :] = head.astype(bf16)
+                if tra is not None:
+                    tra[h, :, rows] = head.T.astype(bf16)
+            split_heads(acc, store)
+    loop(4, qkv_block)
+    ag1.finish()
+
+    ag2 = Gather(at, cr, sems, S_AG2)
+    import_hand_on(3)
+
+    rs1 = Scatter(at, rso, rsi, sems, S_RS1)
+
+    def attend_block(i):
+        slot = at.flip(at.rank, 3 - (((i & 1) << 1) | (i >> 1)))
+        rows = quarter(slot)
+
+        def head(h):
+            st = dot(kn[h], qn[h, rows, :], NT)
+            peak = jnp.max(st, axis=0, keepdims=True)
+            ex = jnp.exp((st - peak) * inv_root)
+            total = jnp.sum(ex, axis=0, keepdims=True)
+            probs = (ex * (1.0 / total)).astype(bf16)
+            lse[h, :, rows] = jnp.broadcast_to(peak * inv_root + jnp.log(total), (8, 256))
+            out = dot(vt[h], probs, NN)
+            mixt[pl.ds(pl.multiple_of(h * HEAD_DIM, 8), HEAD_DIM), :] = out[:HEAD_DIM, :]
+        loop(4, head)
+        low = mixt[...].T[:, :288].astype(bf16)
+        mix[rows, :] = low
+        @pl.when(i == 0)
+        def _():
+            import_wait(1, 3)
+        part = dot(low, wp[...], NN)
+
+        @pl.when(i == 0)
+        def _():
+            rso[0] = part.astype(bf16)
+            rs1.start(0)
+
+        @pl.when(i == 1)
+        def _():
+            rs1.take(0)
+            rso[2] = (part + rsi[0].astype(f32)).astype(bf16)
+            rs1.start(2)
+            pltpu.make_async_copy(cot, cown, sems.at[1, S_C]).wait()
+            cs[...] = cown[...]
+            ag2.start()
+            import_start(7, 8, 9)
+
+        @pl.when(i == 2)
+        def _():
+            rso[1] = part.astype(bf16)
+            rs1.start(1)
+
+        @pl.when(i == 3)
+        def _():
+            own[...] = part
+            import_hand_on(4, 5, 6)
+    mixt[288:, :] = jnp.zeros((96, 256), f32)
+    loop(4, attend_block)
+    ag2.take_sib()
+    ag2.take_nbr()
+    rs1.take(1)
+    rs1.take(2)
+    stats[...] = jnp.zeros(stats.shape, f32)
+
+    def middle_rows(i):
+        rows = pl.ds(pl.multiple_of(i * 32, 32), 32)
+        br = own[rows, :] + rsi[1, rows, :].astype(f32) + rsi[2, rows, :].astype(f32) + obias[0:1, :]
+        branch[rows, :] = br
+        m = xs[rows, :].astype(f32) + mods[gate_attn, :] * br
+        mid[rows, :] = m
+        normed, inv = center_rows(m)
+        n2[rows, :] = normed
+        inv2[rows, :] = jnp.broadcast_to(inv, (32, LANES))
+        target = pl.ds(pl.multiple_of(at.rank * 256 + i * 32, 32), 32)
+        mr[target, :] = (normed * (1.0 + mods[scale_mlp, :]) + mods[shift_mlp, :]).astype(bf16)
+    loop(8, middle_rows)
+    rs1.finish()
+    ag3 = Gather(at, mr, sems, S_AG3)
+    ag3.start()
+
+    ag2.take_diag()
+    ag2.finish()
+    import_wait(3, 4, 5, 6)
+    import_hand_on(7, 8, 9)
+
+    def gate_cot(i):
+        rows = pl.ds(pl.multiple_of(i * 64, 64), 64)
+        cr[rows, :] = (mods[gate_mlp, :] * cr[rows, :].astype(f32)).astype(bf16)
+    loop(16, gate_cot)
+
+    def hgrad_block(i):
+        rows = quarter(i)
+        hgrad[rows, :] = dot(cr[rows, :], w2[...], NT)
+    loop(4, hgrad_block)
+    import_wait(2, 7, 8, 9)
+    rs3 = Scatter(at, rso, rsi, sems, S_RS3)
+
+    def mlp_block(i):
+        slot = slot_of(i)
+        rows = quarter(slot)
+
+        @pl.when(i == 1)
+        def _():
+            ag3.take_sib()
+
+        @pl.when(i == 2)
+        def _():
+            ag3.take_nbr()
+
+        @pl.when(i == 3)
+        def _():
+            ag3.take_diag()
+        big[...] = dot(mr[rows, :], w1[...], NN)
+
+        def act(j):
+            sub = pl.ds(pl.multiple_of(j * 32, 32), 32)
+            full = pl.ds(pl.multiple_of(slot * 256 + j * 32, 32), 32)
+            v = big[sub, :] + bias[0:1, :]
+            v2 = v * v
+            t = jnp.tanh(GELU_A * (v + GELU_B * (v2 * v)))
+            half = 0.5 * (1.0 + t)
+            hid[full, :] = (v * half).astype(bf16)
+            slope = half + 0.5 * v * (1.0 - t * t) * (GELU_A * (1.0 + 3.0 * GELU_B * v2))
+            pg = (hgrad[full, :] * slope).astype(bf16)
+            pgr[full, :] = pg
+            stats[8:9, :] += jnp.sum(pg.astype(f32), axis=0, keepdims=True)
+        loop(8, act)
+        part = dot(pgr[rows, :], w1[...], NT)
+
+        @pl.when(i == 0)
+        def _():
+            own[...] = part
+
+        @pl.when(i == 1)
+        def _():
+            rso[1] = part.astype(bf16)
+            rs3.start(1)
+
+        @pl.when(i == 2)
+        def _():
+            nbrf[...] = part
+
+        @pl.when(i == 3)
+        def _():
+            rso[0] = part.astype(bf16)
+            rs3.start(0)
+    big = stage
+    loop(4, mlp_block)
+    ag3.finish()
+    rs3.take(0)
+
+    def nbr_rows(i):
+        rows = pl.ds(pl.multiple_of(i * 32, 32), 32)
+        rso[2, rows, :] = (nbrf[rows, :] + rsi[0, rows, :].astype(f32)).astype(bf16)
+    loop(8, nbr_rows)
+    rs3.start(2)
+
+    rs2 = Scatter(at, rs2o, rs2i, sems, S_RS2)
+
+    def out_block(i):
+        rows = quarter(at.flip(at.rank, 3 - (((i & 1) << 1) | (i >> 1))))
+        part = dot(hid[rows, :], w2[...], NN)
+
+        @pl.when(i == 0)
+        def _():
+            rs2o[0] = part.astype(bf16)
+            rs2.start(0)
+
+        @pl.when(i == 1)
+        def _():
+            rs2.take(0)
+            mlpz[...] = (part + rs2i[0].astype(f32)).astype(bf16)
+
+        @pl.when(i == 2)
+        def _():
+            rs2o[1] = part.astype(bf16)
+            rs2.start(1)
+
+        @pl.when(i == 3)
+        def _():
+            rs2.take(1)
+            mlpown[...] = part + rs2i[1].astype(f32)
+    loop(4, out_block)
+    rs2.copy(0).wait_send()
+    rs2.copy(1).wait_send()
+    rs3.take(1)
+    rs3.take(2)
+
+    def back_rows(i):
+        rows = pl.ds(pl.multiple_of(i * 32, 32), 32)
+        back = own[rows, :] + rsi[1, rows, :].astype(f32) + rsi[2, rows, :].astype(f32)
+        normed = n2[rows, :]
+        stats[3:4, :] += jnp.sum(back, axis=0, keepdims=True)
+        stats[4:5, :] += jnp.sum(back * normed, axis=0, keepdims=True)
+        u = back * (1.0 + mods[scale_mlp, :])
+        mean_u = jnp.mean(u, axis=1, keepdims=True)
+        mean_p = jnp.mean(u * normed, axis=1, keepdims=True)
+        gout = cs[rows, :].astype(f32)
+        mg = gout + (u - mean_u - normed * mean_p) * inv2[rows, 0:1]
+        mgrad[rows, :] = mg
+        ag = mods[gate_attn, :] * mg
+        stats[2:3, :] += jnp.sum(mg * branch[rows, :], axis=0, keepdims=True)
+        stats[6:7, :] += jnp.sum(ag, axis=0, keepdims=True)
+        stats[7:8, :] += jnp.sum(mods[gate_mlp, :] * gout, axis=0, keepdims=True)
+        target = pl.ds(pl.multiple_of(at.rank * 256 + i * 32, 32), 32)
+        gr[target, :] = ag.astype(bf16)
+    loop(8, back_rows)
+    rs3.finish()
+    ag4 = Gather(at, gr, sems, S_AG4)
+    ag4.start()
+
+    def wgrad(left, right, out, i):
+        cols = pl.ds(pl.multiple_of(i * 128, 128), 128)
+        tile = dot(left[:, cols], right[...], TN).astype(bf16)
+        out[cols, :] = tile
+    loop(9, lambda i: wgrad(mr, pgr, g1, i))
+    loop(9, lambda i: wgrad(cr, hid, g2, i))
+    ag4.take_sib()
+    ag4.take_nbr()
+    ag4.take_diag()
+    ag4.finish()
+    for_mods(lambda cp: cp.wait_send(), None)
+
+    @pl.when(at.away)
+    def _():
+        send(tok, xs, sems, S_X, at.swap).wait_send()
+        send(bblk, bias, sems, S_BIAS, at.swap).wait_send()
+        send(cot, cr.at[quarter(at.r_sib)], sems, S_C, at.swap).wait_send()
+        for i in range(10):
+            import_first(i).wait_send()
+            for k in range(3):
+                import_next(i, k, at.c).wait_send()
+
+
+def call_kf(*args):
+    S, D, H = 1024, 1152, 288
+    V = pltpu.VMEM
+    outs = [((S, D), bf16), ((4, S, 128), bf16), ((4, S, 128), bf16), ((4, S, 128), bf16), ((4, 128, S), bf16), ((4, 8, S), f32),
+            ((S, H), bf16), ((S, D), bf16), ((256, D), f32), ((256, D), bf16), ((256, D), bf16), ((256, D), f32), ((8, D), f32),
+            ((16, D), f32), ((256, D), f32), ((256, D), bf16), ((D, D), bf16), ((D, D), bf16), ((3, D, H), bf16), ((H, D), bf16)]
+    scratch = [V((D, D), bf16), V((D, D), bf16), V((4, 128, S), bf16), V((S, D), bf16), V((S, D), bf16), V((S, D), f32),
+               V((S, D), bf16), V((S, D), bf16), V((3, 256, D), bf16), V((3, 256, D), bf16), V((256, D), f32), V((256, D), f32),
+               V((2, 256, D), bf16), V((2, 256, D), bf16), V((256, D), f32), V((256, D), f32), V((4, 8, D), f32), V((8, D), f32),
+               V((256, 384), f32), V((384, 256), f32), V((256, 128), f32), V((256, D), f32),
+               pltpu.SemaphoreType.DMA((2, N_SEMS)), pltpu.SemaphoreType.DMA((4,))]
+    vm, anys = pl.BlockSpec(memory_space=pltpu.VMEM), pl.BlockSpec(memory_space=pl.ANY)
+    return pl.pallas_call(
+        kf, name="front",
+        out_shape=[jax.ShapeDtypeStruct(s, d) for s, d in outs],
+        in_specs=[anys, anys, vm, vm, vm, anys, anys, anys, anys],
+        out_specs=[vm] * len(outs), scratch_shapes=scratch,
+        compiler_params=pltpu.CompilerParams(collective_id=1, has_side_effects=True, vmem_limit_bytes=67043328),
+    )(*args)
+
+
+T_Z, T_RS4, T_G, T_OUT, T_IG, T_FZ, T_SB, T_GS, T_AL = 0, 1, 4, 13, 14, 15, 21, 24, 27
+N_BACK = 27 + 7
+L_IN = 17
+
+
+def kb(xr_h, qn_h, kn_h, vn_h, kt_h, lse_h, mix_h, gr_h, mgrad_h, xs_h, cs_h, mid_h, mods, stats_h, mlpown_h, mlpz, g1, g2, wq_h, wp_h,
+       obias,
+       out_o, ig_o, w1_o, w2_o, w4_o, al,
+       xr, qn, kn, vn, kt, lse, mix, gr, mgrad, xs, cs, mid, stats, mlpown, wq, wp,
+       don, dh, dense, dka, dva, rso, rsi, own, rs2z, g4, rg1, rg2, rg4, gown, half, half4, keep, keep4, fz, fz4, sb, sb4,
+       outb, igb, acc, gs, lb, sems, lsem):
+    at = Spot()
+    inv_root = 1.0 / math.sqrt(HEAD_DIM)
+    far = (at.dp, at.flip(at.z, 2))
+    diag = (at.flip(at.dp, 1), at.flip(at.z, 1))
+    spread = [*at.peers, far, *[(at.flip(at.dp, 2 * k), at.flip(at.z, 2)) for k in (1, 2, 3)]]
+    entry(at, [far, diag, *spread[4:]])
+
+    loads = [(gr_h, gr), (wp_h, wp), (kn_h, kn), (qn_h, qn), (vn_h, vn), (kt_h, kt), (lse_h, lse), (wq_h, wq), (xr_h, xr), (mix_h, mix),
+             (mgrad_h, mgrad), (xs_h, xs), (cs_h, cs), (mid_h, mid), (stats_h, stats), (mlpown_h, mlpown)]
+    for i, (a, b) in enumerate(loads):
+        pltpu.make_async_copy(a, b, lsem.at[i]).start()
+
+    def have(*indices):
+        for i in indices:
+            pltpu.make_async_copy(loads[i][0], loads[i][1], lsem.at[i]).wait()
+
+    zcopy = send(mlpz, rs2z, sems, T_Z, at.nbr)
+    zcopy.start()
+
+    def slice_rows(slot, size=288):
+        return pl.ds(pl.multiple_of(slot * size, 16), size)
+
+    def gcopy(m, k):
+        rows = slice_rows(at.flip(at.c, k + 1))
+        if m == 2:
+            return send(g4.at[:, rows, :], rg4.at[k], sems, T_G + 6 + k, at.peers[k])
+        return send((g1, g2)[m].at[rows, :], (rg1, rg2)[m].at[k], sems, T_G + 3 * m + k, at.peers[k])
+
+    for m in range(2):
+        for k in range(3):
+            gcopy(m, k).start()
+        mine = pltpu.make_async_copy((g1, g2)[m].at[slice_rows(at.c), :], gown.at[m], lsem.at[16 + m])
+        mine.start()
+
+    have(0, 1)
+
+    def mix_block(i):
+        rows = quarter(i)
+        acc[:, :288] = dot(gr[rows, :], wp[...], NT)
+
+        def store(h, head):
+            don[h, rows, :] = head.astype(bf16)
+        split_heads(acc, store)
+    loop(4, mix_block)
+    have(2, 3, 4, 5, 6)
+
+    def back_head(h):
+        dka[...] = jnp.zeros(dka.shape, f32)
+        dva[...] = jnp.zeros(dva.shape, f32)
+
+        def back_block(i):
+            rows = quarter(i)
+            qb, db = qn[h, rows, :], don[h, rows, :]
+            st = dot(kn[h], qb, NT)
+            probs = jnp.exp(st * inv_root - lse[h, 0:1, rows])
+            dp = dot(vn[h], db, NT)
+            row = jnp.sum(probs * dp, axis=0, keepdims=True)
+            ds = (probs * (dp - row)).astype(bf16)
+            dqt = dot(kt[h], ds, NN) * inv_root
+            dh[0, h, rows, :] = dqt.T.astype(bf16)
+            dka[...] += dot(ds, qb, NN)
+            dva[...] += dot(probs.astype(bf16), db, NN)
+        loop(4, back_block)
+        dh[1, h] = (dka[...] * inv_root).astype(bf16)
+        dh[2, h] = dva[...].astype(bf16)
+    loop(4, back_head)
+    have(7)
+    rs4 = Scatter(at, rso, rsi, sems, T_RS4)
+
+    def back_part(i):
+        rows = quarter(at.flip(at.rank, 3 - (((i & 1) << 1) | (i >> 1))))
+        for t in range(3):
+            dense[t, rows, :] = join_heads([dh[t, h, rows, :].astype(f32) for h in range(4)]).astype(bf16)
+        part = dot(dense[0, rows, :], wq[0], NT)
+        part += dot(dense[1, rows, :], wq[1], NT)
+        part += dot(dense[2, rows, :], wq[2], NT)
+
+        @pl.when(i == 0)
+        def _():
+            rso[0] = part.astype(bf16)
+            rs4.start(0)
+
+        @pl.when(i == 1)
+        def _():
+            rs4.take(0)
+            rso[2] = (part + rsi[0].astype(f32)).astype(bf16)
+            rs4.start(2)
+
+        @pl.when(i == 2)
+        def _():
+            rso[1] = part.astype(bf16)
+            rs4.start(1)
+
+        @pl.when(i == 3)
+        def _():
+            own[...] = part
+    loop(4, back_part)
+
+    have(8, 9)
+
+    def wgrad(i):
+        cols = pl.ds(pl.multiple_of(i * 128, 128), 128)
+        g4[0, cols, :] = dot(gr[:, cols], mix[...], TN).astype(bf16)
+        for t in range(3):
+            g4[1 + t, cols, :] = dot(xr[:, cols], dense[t], TN).astype(bf16)
+    loop(9, wgrad)
+    for k in range(3):
+        gcopy(2, k).start()
+    have(10, 11, 12, 13, 14, 15)
+    for row, t in ((9, 0), (10, 2)):
+        stats[row:row + 1, :288] = jnp.sum(dense[t].astype(f32), axis=0, keepdims=True)
+
+    zcopy.wait_recv()
+    gate_mlp = mods[5:6, :]
+
+    def out_rows(i):
+        rows = pl.ds(pl.multiple_of(i * 32, 32), 32)
+        br = mlpown[rows, :] + rs2z[rows, :].astype(f32) + obias[1:2, :]
+        stats[5:6, :] += jnp.sum(cs[rows, :].astype(f32) * br, axis=0, keepdims=True)
+        outb[rows, :] = (mid[rows, :] + gate_mlp * br).astype(bf16)
+    loop(8, out_rows)
+
+    @pl.when(at.away)
+    def _():
+        send(outb, out_o, sems, T_OUT, at.swap).start()
+
+    @pl.when(at.home)
+    def _():
+        out_o[...] = outb[...]
+
+    rs4.take(1)
+    rs4.take(2)
+    scale_attn = mods[1:2, :]
+
+    def in_rows(i):
+        rows = pl.ds(pl.multiple_of(i * 32, 32), 32)
+        back = own[rows, :] + rsi[1, rows, :].astype(f32) + rsi[2, rows, :].astype(f32)
+        normed, inv = center_rows(xs[rows, :].astype(f32))
+        stats[0:1, :] += jnp.sum(back, axis=0, keepdims=True)
+        stats[1:2, :] += jnp.sum(back * normed, axis=0, keepdims=True)
+        w = back * (1.0 + scale_attn)
+        mean_w = jnp.mean(w, axis=1, keepdims=True)
+        mean_p = jnp.mean(w * normed, axis=1, keepdims=True)
+        total = mgrad[rows, :] + (w - mean_w - normed * mean_p) * inv
+        ig_o[rows, :] = total
+        igb[0, rows, :] = total.astype(bf16)
+    loop(8, in_rows)
+
+    @pl.when(at.away)
+    def _():
+        send(igb.at[0], igb.at[1], sems, T_IG, at.swap).start()
+
+    gs[0] = stats[...]
+    mates = [at.sib, at.nbr, diag]
+
+    def gs_copy(k):
+        return send(gs.at[0], gs.at[k + 1], sems, T_GS + k, mates[k])
+    for k in range(3):
+        gs_copy(k).start()
+
+    def reduce_matrix(m):
+        mine = pltpu.make_async_copy((g1, g2)[m].at[slice_rows(at.c), :], gown.at[m], lsem.at[16 + m])
+        mine.wait()
+        into = (rg1, rg2)[m]
+        for k in range(3):
+            send(gown.at[m], into.at[k], sems, T_G + 3 * m + k, at.peers[k]).wait_recv()
+
+        def add(i):
+            for h in range(2):
+                rows = pl.ds(pl.multiple_of(h * 144 + i * 16, 16), 16)
+                part = pl.ds(pl.multiple_of(i * 16, 16), 16)
+                total = (gown[m, rows, :].astype(f32) + into[0, rows, :].astype(f32)
+                         + into[1, rows, :].astype(f32) + into[2, rows, :].astype(f32))
+                half[m, h, part, :] = total.astype(bf16)
+
+                @pl.when(at.q == h)
+                def _():
+                    keep[m, part, :] = total
+        loop(9, add)
+
+    def reduce_last():
+        for k in range(3):
+            send(g4.at[:, slice_rows(at.c), :], rg4.at[k], sems, T_G + 6 + k, at.peers[k]).wait_recv()
+
+        def add(i):
+            for t in range(4):
+                for h in range(2):
+                    rows = pl.ds(pl.multiple_of(h * 144 + i * 16, 16), 16)
+                    part = pl.ds(pl.multiple_of(i * 16, 16), 16)
+                    full = pl.ds(pl.multiple_of(at.c * 288 + h * 144 + i * 16, 16), 16)
+                    total = (g4[t, full, :].astype(f32) + rg4[0, t, rows, :].astype(f32)
+                             + rg4[1, t, rows, :].astype(f32) + rg4[2, t, rows, :].astype(f32))
+                    half4[h, t, part, :] = total.astype(bf16)
+
+                    @pl.when(at.q == h)
+                    def _():
+                        keep4[t, part, :] = total
+        loop(9, add)
+
+    def home_copies(m, other, same):
+        src = half4 if m == 2 else half.at[m]
+        z_to, s_to = (fz4, sb4) if m == 2 else (fz.at[m], sb.at[m])
+        return (send(src.at[other], s_to, sems, T_SB + m, at.sib),
+                send(src.at[same], z_to, sems, T_FZ + m, far),
+                send(src.at[other], z_to, sems, T_FZ + 3 + m, at.swap))
+
+    def hand_home(m, what):
+        to_sib, to_far, to_swap = home_copies(m, 1 - at.q, at.q)
+
+        @pl.when(at.home)
+        def _():
+            what(to_sib)
+
+        @pl.when(at.away)
+        def _():
+            what(to_far)
+            what(to_swap)
+
+    def arrive(m):
+        to_sib, to_far, to_swap = home_copies(m, 1 - at.q, at.q)
+
+        @pl.when(at.home)
+        def _():
+            to_far.wait_recv()
+
+        @pl.when(at.away)
+        def _():
+            to_sib.wait_recv()
+            to_swap.wait_recv()
+
+    for m in range(2):
+        reduce_matrix(m)
+        hand_home(m, lambda cp: cp.start())
+
+    for k in range(3):
+        gs_copy(k).wait_recv()
+    lb[0:8, :] = gs[0, 0:8, :] + gs[1, 0:8, :] + gs[2, 0:8, :] + gs[3, 0:8, :]
+    for k, bits in enumerate((0, 2, 1, 3)):
+        for rank in range(4):
+            @pl.when(at.flip(at.rank, bits) == rank)
+            def _():
+                lb[8 + 3 * rank:11 + 3 * rank, :] = gs[k, 8:11, :]
+    lb[20:22, :] = mods[6:8, :]
+    latent = at.dp - at.q + at.g
+
+    def al_copy(k):
+        return send(lb, al.at[latent], sems, T_AL + k, spread[k])
+    for k in range(7):
+        al_copy(k).start()
+    al[latent] = lb[...]
+
+    reduce_last()
+    hand_home(2, lambda cp: cp.start())
+    for m in range(2):
+        arrive(m)
+
+        @pl.when(at.home)
+        def _():
+            (w1_o, w2_o)[m][...] = keep[m] + fz[m].astype(f32)
+
+        @pl.when(at.away)
+        def _():
+            (w1_o, w2_o)[m][...] = sb[m].astype(f32) + fz[m].astype(f32)
+
+    @pl.when(at.away)
+    def _():
+        send(outb, out_o, sems, T_OUT, at.swap).wait()
+        send(igb.at[0], igb.at[1], sems, T_IG, at.swap).wait()
+
+        def widen(i):
+            rows = pl.ds(pl.multiple_of(i * 32, 32), 32)
+            ig_o[rows, :] = igb[1, rows, :].astype(f32)
+        loop(8, widen)
+    arrive(2)
+
+    @pl.when(at.home)
+    def _():
+        w4_o[...] = keep4[...] + fz4[...].astype(f32)
+
+    @pl.when(at.away)
+    def _():
+        w4_o[...] = sb4[...].astype(f32) + fz4[...].astype(f32)
+    for k in range(7):
+        al_copy(k).wait_recv()
+    zcopy.wait_send()
+    rs4.finish()
+    for m in range(3):
+        for k in range(3):
+            gcopy(m, k).wait_send()
+        hand_home(m, lambda cp: cp.wait_send())
+    for k in range(3):
+        gs_copy(k).wait_send()
+    for k in range(7):
+        al_copy(k).wait_send()
+
+
+def call_kb(*args):
+    S, D, H = 1024, 1152, 288
+    V = pltpu.VMEM
+    outs = [((256, D), bf16), ((256, D), f32), ((144, D), f32), ((144, D), f32), ((4, 144, H), f32), ((8, 24, D), f32)]
+    scratch = [V((S, D), bf16), V((4, S, 128), bf16), V((4, S, 128), bf16), V((4, S, 128), bf16), V((4, 128, S), bf16), V((4, 8, S), f32),
+               V((S, H), bf16), V((S, D), bf16), V((256, D), f32), V((256, D), bf16), V((256, D), bf16), V((256, D), f32), V((16, D), f32),
+               V((256, D), f32), V((3, D, H), bf16), V((H, D), bf16),
+               V((4, S, 128), bf16), V((3, 4, S, 128), bf16), V((3, S, H), bf16), V((S, 128), f32), V((S, 128), f32),
+               V((3, 256, D), bf16), V((3, 256, D), bf16), V((256, D), f32), V((256, D), bf16),
+               V((4, D, H), bf16), V((3, H, D), bf16), V((3, H, D), bf16), V((3, 4, H, H), bf16), V((2, H, D), bf16),
+               V((2, 2, 144, D), bf16), V((2, 4, 144, H), bf16), V((2, 144, D), f32), V((4, 144, H), f32),
+               V((2, 144, D), bf16), V((4, 144, H), bf16), V((2, 144, D), bf16), V((4, 144, H), bf16),
+               V((256, D), bf16), V((2, 256, D), bf16), V((256, 384), f32), V((4, 16, D), f32), V((24, D), f32),
+               pltpu.SemaphoreType.DMA((2, N_BACK)), pltpu.SemaphoreType.DMA((18,))]
+    vm, anys = pl.BlockSpec(memory_space=pltpu.VMEM), pl.BlockSpec(memory_space=pl.ANY)
+    specs = [anys] * 12 + [vm] + [anys] * 2 + [anys] + [anys] * 4 + [vm]
+    return pl.pallas_call(
+        kb, name="back",
+        out_shape=[jax.ShapeDtypeStruct(s, d) for s, d in outs],
+        in_specs=specs, out_specs=[vm] * len(outs), scratch_shapes=scratch,
+        compiler_params=pltpu.CompilerParams(collective_id=2, has_side_effects=True, vmem_limit_bytes=67043328),
+    )(*args)
+
+
+def kc(part, all_o, sems):
+    at = Spot()
+    barrier = pltpu.get_barrier_semaphore()
+    mates = [(at.dp, at.flip(at.z, k)) for k in (1, 2, 3)]
+    for mate in mates:
+        pl.semaphore_signal(barrier, inc=1, device_id=mate, device_id_type=MESH)
+    pl.semaphore_wait(barrier, 3)
+    copies = [send(part, all_o.at[k + 1], sems, k, mates[k]) for k in range(3)]
+    for cp in copies:
+        cp.start()
+    all_o[0] = part[...]
+    for cp in copies:
+        cp.wait()
+
+
+def call_kc(part):
+    vm = pl.BlockSpec(memory_space=pltpu.VMEM)
+    return pl.pallas_call(
+        kc, name="small", out_shape=jax.ShapeDtypeStruct((4, *part.shape), f32), in_specs=[vm], out_specs=vm,
+        scratch_shapes=[pltpu.SemaphoreType.DMA((2, 3))],
+        compiler_params=pltpu.CompilerParams(collective_id=3, has_side_effects=True),
+    )(part)
+
+
+def fast_body(tokens, labels, timesteps, label_table, ada_weight, ada_bias, qkv_weight, qv_bias, proj_weight, out_bias, fc1_weight,
+              fc1_bias, fc2_weight, cotangent):
+    width, cols = tokens.shape[2], ada_weight.shape[1]
+    dp_rank, z_rank = lax.axis_index("dp"), lax.axis_index("tensor")
+    cond = label_table[labels].astype(f32) + time_features(timesteps, width)
+    cond_low = jax.nn.silu(cond).astype(bf16)
+    mod = jnp.dot(cond_low, ada_weight, preferred_element_type=f32) + ada_bias
+    third = cols // 3
+    mblk = jnp.concatenate([
+        jnp.pad(mod.reshape(3, third), ((0, 0), (0, width - third))), cond,
+        jnp.broadcast_to(labels.astype(f32)[:, None], (1, width)), jnp.zeros((3, width), f32)])
+    bblk = jnp.concatenate([fc1_bias[None], jnp.pad(qv_bias, ((0, 0), (0, width - qv_bias.shape[1]))), jnp.zeros((5, width), f32)])
+    front = call_kf(tokens[0], cotangent[0], mblk, bblk, out_bias, qkv_weight, proj_weight, fc1_weight, fc2_weight)
+    output, input_grad, w1, w2, w4, al = call_kb(*front, out_bias)
+    mod_all = al[:, :6].reshape(8, 6 * width)
+    mod_cols = lax.dynamic_slice_in_dim(mod_all, z_rank * cols, cols, 1)
+    terms = jnp.dot(mod_cols, ada_weight.astype(f32).T, precision=lax.Precision.HIGHEST)
+    silu_grad = jnp.sum(call_kc(terms), axis=0)
+    cond_all, label_all = al[:, 20], al[:, 21, 0].astype(jnp.int32)
+    low_all, silu_pull = jax.vjp(jax.nn.silu, cond_all)
+    cond_grad = silu_pull(silu_grad)[0]
+    low_all = low_all.astype(bf16).astype(f32)
+    rows = width // lax.axis_size("dp")
+    low_rows = lax.dynamic_slice_in_dim(low_all, dp_rank * rows, rows, 1)
+    ada_grad = sum(low_rows[n][:, None] * mod_cols[n][None, :] for n in range(8))
+    ada_bias_grad = lax.dynamic_slice_in_dim(jnp.sum(mod_cols, axis=0), dp_rank * (cols // 8), cols // 8, 0)
+    class_ids = jnp.arange(label_table.shape[0], dtype=jnp.int32)
+    table_grad = sum(jnp.where((class_ids == label_all[n])[:, None], cond_grad[n][None, :], 0.0) for n in range(8))
+    sums = jnp.sum(al, axis=0)
+    out_bias_grad = sums[6:8]
+    ranks = sums[8:20].reshape(4, 3, width)
+    qv_grad = jnp.moveaxis(ranks[:, 1:3, :width // 4], 0, 1).reshape(2, width)
+    fc1_bias_grad = lax.dynamic_slice(ranks[:, 0], (z_rank, dp_rank * rows), (1, rows))[0]
+    return (output[None], input_grad[None], table_grad, ada_grad, ada_bias_grad, w4[1:], qv_grad, w4[0].T, out_bias_grad, w1, fc1_bias_grad, w2.T)
+
+
 def solution(mesh):
     placed = (
         P("dp", "tensor", None),
@@ -310,8 +1246,9 @@
         P("tensor", None),
         P("dp", "tensor", None),
     )
+    small = mesh.shape["dp"] == 8 and mesh.shape["tensor"] == 4
     return jax.shard_map(
-        body,
+        fast_body if small else body,
         mesh=mesh,
         in_specs=placed,
         out_specs=(

time: 833 us -> 372 us (0.45)
  waiting for transfers between devices: 503 us -> 0 us
  Pallas kernels: 0 us -> 330 us
  matrix products: 118 us -> 7.77 us
  blocking collectives: 96.7 us -> 0 us
  local copies, waits for them, and re-layouts: 46.1 us -> 13.8 us
  other arithmetic: 33.4 us -> 15.3 us
  between operations: 17.7 us -> 2.41 us
    pallas_call x0 -> x3, Pallas kernels: none -> 330 us  [the longest x1 185 us: call_kf(): pl.pallas_call(kf, name='front', out_shape=[jax.ShapeDtypeStruct(s, d) fo...]
    reduce_scatter x7 -> x0, waiting for transfers between devices: 312 us -> none  [the longest x1 60.7 us: body(): lax.psum_scatter(fc1_grad, 'dp', scatter_dimension=0, tiled=True)]
    all_gather x4 -> x0, waiting for transfers between devices: 191 us -> none  [the longest x1 51.9 us: body(): attn_rows = lax.all_gather(attn_input, 'tensor', axis=1, tiled=True)]
    dot_general x36 -> x2, matrix products: 118 us -> 7.77 us  [the longest x1 4.47 us: fast_body(): jnp.dot(mod_cols, ada_weight.astype(f32).T, precision=lax.Precision.HIGHEST)]
    psum x2 -> x0, blocking collectives: 56.3 us -> none  [the longest x1 42.1 us: body(): lax.psum((out_bias_part, qv_full), ('dp', 'tensor'))]
    unnamed x2 -> x0, blocking collectives: 29.8 us -> none
    unnamed x96 -> x26, local copies, waits for them, and re-layouts: 35.4 us -> 8.32 us
    reduce_sum x12 -> x3, other arithmetic: 16.4 us -> 1.06 us  [the longest x1 0.93 us: fast_body(): silu_grad = jnp.sum(call_kc(terms), axis=0)]
  transfers between devices with their start and end apart: 13 -> 0, of which waited for: 11 -> 0; matrix products, arithmetic and copies ran while one was open for 11% -> 0% of each run, Pallas kernels for 0% -> 0%
where the time goes in v2:
time: 372 us; the launch traced here: 369 us
  Pallas kernels  330 us (89%)
  other arithmetic  15.3 us (4%)
  local copies, waits for them, and re-layouts  13.8 us (4%)
  matrix products  7.77 us (2%)
    pallas_call x1, Pallas kernels, call_kf(): pl.pallas_call(kf, name='front', out_shape=[jax.ShapeDtypeStruct(s, d) fo...  185 us
    pallas_call x1, Pallas kernels, call_kb(): pl.pallas_call(kb, name='back', out_shape=[jax.ShapeDtypeStruct(s, d) for...  138 us
    unnamed x26, local copies, waits for them, and re-layouts  8.32 us

profile of v2, /device:TPU:1, one launch (start us, length us, event | category | flops | bytes accessed | tf_op | source)
XLA Modules:
  0.0 368.9 jit_solution(12478377035725978886)
XLA Ops:
  0.6 0.0 copy-start.6
  0.7 0.0 copy-start
  2.2 0.8 maximum_add_fusion.1
  3.0 0.1 multiply_convert_fusion
  3.1 0.0 copy-start.7
  3.1 0.0 copy-start.8
  3.1 3.3 convolution_reduce_fusion
  6.4 0.0 copy-done.6
  6.4 0.1 reshape.159
  6.5 0.1 pad.17.clone
  6.6 0.1 pad.18.clone
  6.7 0.7 fusion.6.mblk
  7.4 0.0 copy-done
  7.4 2.6 copy.29.wqkv
  9.9 0.0 copy-done.7
  9.9 0.1 pad.14.clone
  10.0 0.0 copy-done.8
  10.0 0.7 fusion.4.bblk
  10.7 184.7 %front.1 = (bf16[1024,1152]{1,0:T(8,128)(2,1)}, bf16[4,1024,128]{2,1,0:T(8,128)(2,1)}, bf16[4,1024,128]{2,1,0:T(8,128)(2,1)}, bf16[4,1024,128]{2,1,0:T(8,128)(2,...) custom-call(bf16[256,1152]{1,0:T(8,128)(2,1)} %bitcast.51, ...), custom_call_target="tpu_custom_call" | custom-call | tf_op jit(solution)/shard_map/front/pallas_call | solution.py:832
  195.4 138.0 %back.1 = (bf16[256,1152]{1,0:T(8,128)(2,1)}, f32[256,1152]{1,0:T(8,128)}, f32[144,1152]{1,0:T(8,128)}, f32[144,1152]{1,0:T(8,128)}, f32[4,144,288]{2,1,0:T(8,128)}, /*index=5*/f32[8,24,1152]{2,1,0:T(8,128)}) custom-call(bf16[1024,1152]{1,0:T(8,128)(2,1)} %get-tuple-element.38.xr_h, bf16[4,1024,128]{2,1,0:T(8,128)(2,1)} %get-tuple-element.39.qn_h, ...), custom_call_target="tpu_custom_call" | custom-call | tf_op jit(solution)/shard_map/back/pallas_call | solution.py:1164
  333.4 0.0 copy-start.1
  333.4 1.1 slice_bitcast_fusion
  334.6 4.5 %fusion.part = f32[8,1152]{1,0:T(8,128)} fusion(bf16[1152,1728]{0,1:T(8,128)(2,1)} %param.18, f32[8,6912]{1,0:T(8,128)S(1)} %bitcast.47, s32[]{:T(128)S(6)} %select_n.42), kind=kOutput, calls=%fused_computation.7 | convolution fusion | flops 191102976 | bytes 4075524 | tf_op jit(solution)/shard_map/dot_general | solution.py:1212
  339.0 0.0 copy-start.3
  339.0 7.0 %small.1 = f32[4,8,1152]{2,1,0:T(8,128)} custom-call(f32[8,1152]{1,0:T(8,128)} %fusion.part), custom_call_target="tpu_custom_call" | custom-call | tf_op jit(solution)/shard_map/small/pallas_call | solution.py:1189
  346.0 0.9 reduce_sum.27
  346.9 0.0 copy-done.1
  347.0 0.1 fusion.9
  347.1 0.2 dynamic-slice_reduce_fusion.8
  347.3 1.6 multiply_add_fusion
  349.0 0.1 slice_reduce_fusion.7
  349.1 0.5 fusion.14
  349.6 0.6 iota_compare_fusion.2
  350.3 0.7 iota_compare_fusion.3
  351.0 0.7 iota_compare_fusion.4
  351.6 0.7 iota_compare_fusion.5
  352.3 0.7 iota_compare_fusion.6
  352.9 0.7 iota_compare_fusion.7
  353.6 0.7 iota_compare_fusion.8
  354.2 0.7 iota_compare_fusion.9
  354.9 0.0 copy-start.2
  354.9 4.9 %select_add_fusion = f32[1001,1152]{1,0:T(8,128)} fusion(f32[1152]{0:T(1024)S(1)} %get-tuple-element.84, f32[1152]{0:T(1024)S(1)} %get-tuple-element.85, f32[1152]{0:T(1024)S(1)} %get-tuple-element.86, f32[1152]{0:T(1024)S(1)} %get-tuple-element.87, f32[1152]{0:T(1024)S(1)} %get-tuple-element.88, f32[1152]{0:T(1024)S(1)} %get-tuple-element.89, ...), kind=kLoop, calls=%fused_computation | loop fusion | flops 17297280 | bytes 4657480 | tf_op jit(solution)/shard_map/add | solution.py:1223
  359.9 0.0 copy-done.3
  359.9 0.9 slice.166
  360.7 0.1 dynamic-slice_reduce_fusion
  360.8 0.6 dynamic_slice.14
  361.5 0.0 copy-start.4
  361.6 0.6 constant_dynamic-slice_fusion
  362.3 0.7 reshape.162
  363.0 0.0 copy-start.5
  363.0 0.7 slice_bitcast_fusion.1
  363.7 0.6 slice.205
  364.3 1.9 copy.47
  366.2 0.0 copy-done.2
  366.2 1.0 copy.48
  367.2 0.0 copy-done.5
  367.2 0.8 copy.49
  368.1 0.0 copy-done.4
  368.1 0.8 copy.50
  (20 shorter events, 0.3 us)
Async XLA Ops:
  0.6 5.8 %copy-start.6 = (f32[1728]{0:T(1024)S(1)}, f32[1728]{0:T(1024)}, u32[]{:S(2)}) copy-start(f32[1728]{0:T(1024)} %param.19) | copy-start | bytes 20740
  0.7 6.7 %copy-start = (bf16[3,1152,288]{1,2,0:T(8,128)(2,1)S(1)}, bf16[3,1152,288]{1,2,0:T(8,128)(2,1)}, u32[]{:S(2)}) copy-start(bf16[3,1152,288]{1,2,0:T(8,128)(2,1)} %param.20) | copy-start | bytes 5971972
  3.1 6.8 %copy-start.7 = (f32[1152]{0:T(1024)S(1)}, f32[1152]{0:T(1024)}, u32[]{:S(2)}) copy-start(f32[1152]{0:T(1024)} %param.25) | copy-start | bytes 13828
  3.1 6.9 %copy-start.8 = (f32[2,288]{1,0:T(2,128)S(1)}, f32[2,288]{1,0:T(2,128)}, u32[]{:S(2)}) copy-start(f32[2,288]{1,0:T(2,128)} %param.21) | copy-start | bytes 6916
  333.4 13.5 %copy-start.1 = (f32[8,24,1152]{2,1,0:T(8,128)S(1)}, f32[8,24,1152]{2,1,0:T(8,128)}, u32[]{:S(2)}) copy-start(f32[8,24,1152]{2,1,0:T(8,128)} %get-tuple-element.60) | copy-start | bytes 2654212
  339.0 20.8 %copy-start.3 = (f32[4,144,288]{2,1,0:T(8,128)S(1)}, f32[4,144,288]{2,1,0:T(8,128)}, u32[]{:S(2)}) copy-start(f32[4,144,288]{2,1,0:T(8,128)} %get-tuple-element.61) | copy-start | bytes 1990660
  354.9 11.3 %copy-start.2 = (f32[256,1152]{1,0:T(8,128)S(1)}, f32[256,1152]{1,0:T(8,128)}, u32[]{:S(2)}) copy-start(f32[256,1152]{1,0:T(8,128)} %get-tuple-element.59) | copy-start | bytes 3538948
  361.5 6.5 %copy-start.4 = (f32[144,1152]{1,0:T(8,128)S(1)}, f32[144,1152]{1,0:T(8,128)}, u32[]{:S(2)}) copy-start(f32[144,1152]{1,0:T(8,128)} %get-tuple-element.63) | copy-start | bytes 1990660
  363.0 4.2 %copy-start.5 = (f32[144,1152]{1,0:T(8,128)S(1)}, f32[144,1152]{1,0:T(8,128)}, u32[]{:S(2)}) copy-start(f32[144,1152]{1,0:T(8,128)} %get-tuple-element.134) | copy-start | bytes 1990660
